TPU v7x, 32 devices: a whole 2x2x4 slice. The times are simulated.
32 devices in a mesh: gx: 4 (over z), gy: 4 (over y, core), gz: 2 (over x).
Axes of the slice: x: 2, y: 2, z: 4, core: 2. Of those that a mesh axis runs over, the one named last changes fastest.
Arguments:
- solution: float32 [64, 64, 256], P('gx', 'gy', 'gz'), may hold values from -6 to 6
- right_side: float32 [64, 64, 256], P('gx', 'gy', 'gz'), may hold values from -6 to 6
Outputs:
- improved: float32 [64, 64, 256], P('gx', 'gy', 'gz')
All inputs are finite; a program needn't handle non-finite values.
Results may differ from a plain program's by a relative error of at most 0.00015.
Values sent between devices are 32-bit elements; how exact they have to be, the bound alone decides.
A program may use at most 64 MiB of HBM per device.

v0:
```python
import functools

import jax
import jax.numpy as jnp
import numpy as np
from jax import lax
from jax.experimental import pallas as pl
from jax.experimental.pallas import tpu as pltpu
from jax.sharding import PartitionSpec as P

F32 = jnp.float32
BF16 = jnp.bfloat16
MESH = pl.DeviceIdType.MESH
H = 8
ZR = 32
REACH = 3

RHO0 = 1.0 / 1.2
RHO1 = 1.0 / (2.4 - RHO0)
FIRST = 1.0 / 1.32
KEEP = RHO1 * RHO0
STEP = 2.0 * RHO1 / 1.1


def restrict_taps(g):
    if g % 2 == 0:
        return ((-3, -0.125), (-1, 0.375), (0, 1.0), (1, 0.375), (3, -0.125))
    return ((-1, 0.75), (0, 1.0), (1, 0.75))


def prolong_taps(f):
    if f % 2 == 0:
        return ((f // 2, 1.0),)
    q = f // 4
    if f % 4 == 1:
        return ((2 * q, 0.375), (2 * q + 1, 0.75), (2 * q + 2, -0.125))
    return ((2 * q, -0.125), (2 * q + 1, 0.75), (2 * q + 2, 0.375))


def transfer(taps, outs, out_pos, in_pos, n_out, n_in, scale):
    m = np.zeros((n_out, n_in), np.float32)
    for o in outs:
        for s, w in taps(o):
            row, col = out_pos(o), in_pos(scale * o + s if scale else s)
            if col is not None and 0 <= col < n_in:
                m[row, col] += w
    return m


def zdot(v, w):
    hi = v.astype(BF16)
    lo = (v - hi.astype(F32)).astype(BF16)
    return jnp.dot(hi, w, preferred_element_type=F32) + jnp.dot(
        lo, w, preferred_element_type=F32
    )


def exact(a, b):
    return jnp.dot(a, b, preferred_element_type=F32, precision=lax.Precision.HIGHEST)


def z_filters(v):
    lanes = v.shape[1]
    even = lax.broadcasted_iota(jnp.int32, v.shape, 1) % 2 == 0
    s1 = pltpu.roll(v, 1, 1) + pltpu.roll(v, lanes - 1, 1)
    s2 = jnp.where(even, pltpu.roll(v, 2, 1) + pltpu.roll(v, lanes - 2, 1), 0.0)
    m = jnp.where(even, 8.0, 16.0) * v + 2.0 * s1 - s2
    w = jnp.where(even, -2.0, -16.0) * v - 12.0 * s1 + 3.0 * s2
    return m, w


def kernel(
    geo, u_ref, b_ref, rz0, ry0, rz1, ry1, pz1, py1, pz0, py0, out_ref,
    ue, be, d0, r0, a0, c0, packs, unpacks, y0, y1, y2, blk, zin, g1, d1, r1, s1, a1, c1,
    r2, d2, a2, t2, send, recv, zsend, zrecv, gsend, grecv, gzsend, gzrecv,
):
    nx, ny, nz, bx, by, bz, wx, wy = geo
    ix, iy, iz = lax.axis_index("gx"), lax.axis_index("gy"), lax.axis_index("gz")
    full_x, full_y = wx == nx, wy == ny
    cx, cy, cz = bx // 2, by // 2, bz // 2
    start_x = 0 if full_x else ix - REACH
    start_y = 0 if full_y else iy - REACH

    def at(axis, off):
        return (
            ix + off if axis == 0 else ix,
            iy + off if axis == 1 else iy,
            iz + off if axis == 2 else iz,
        )

    place = (ix, iy, iz)
    counts = (nx, ny, nz)

    def there(axis, off):
        pos = place[axis] + off
        return (pos >= 0) & (pos < counts[axis])

    spans = (wx - 1 if full_x else REACH, wy - 1 if full_y else REACH, 1 if nz > 1 else 0)
    offsets = [[o for o in range(-s, s + 1) if o] for s in spans]

    ue[...] = jnp.zeros_like(ue)
    be[...] = jnp.zeros_like(be)
    unpacks[...] = jnp.zeros_like(unpacks)
    y0[...] = jnp.zeros_like(y0)
    zin[...] = jnp.zeros_like(zin)
    g1[...] = jnp.zeros_like(g1)
    ue[H : H + bx, H : H + by, :bz] = u_ref[...]
    be[H : H + bx, H : H + by, :bz] = b_ref[...]

    barrier = pltpu.get_barrier_semaphore()
    total = 0
    for axis in range(3):
        for off in offsets[axis]:
            ok = there(axis, off)
            total = total + ok.astype(jnp.int32)

            @pl.when(ok)
            def _():
                pl.semaphore_signal(
                    barrier, inc=1, device_id=at(axis, off), device_id_type=MESH
                )

    pl.semaphore_wait(barrier, total)

    def remote(src, dst, ss, rs, axis, off):
        return pltpu.make_async_remote_copy(
            src_ref=src, dst_ref=dst, send_sem=ss, recv_sem=rs,
            device_id=at(axis, off), device_id_type=MESH,
        )

    def start_if(axis, off, copies):
        @pl.when(there(axis, off))
        def _():
            for c in copies:
                c.start()

    def recv_if(axis, off, copies):
        @pl.when(there(axis, -off))
        def _():
            for c in copies:
                c.wait_recv()

    def sent_if(axis, off, copies):
        @pl.when(there(axis, off))
        def _():
            for c in copies:
                c.wait_send()

    L = bz

    def x_copies(off):
        res = []
        for n, (ref, ext, w) in enumerate(((u_ref, ue, H), (b_ref, be, H - 2))):
            k = n * 2 + (off > 0)
            lo = bx - w if off > 0 else 0
            dst = H - w if off > 0 else H + bx
            res.append(
                remote(
                    ref.at[lo : lo + w],
                    ext.at[dst : dst + w, H : H + by, :L],
                    send.at[k], recv.at[k], 0, off,
                )
            )
        return res

    def y_copies(off):
        res = []
        for n, (ref, ext) in enumerate(((u_ref, ue), (b_ref, be))):
            k = 4 + n * 2 + (off > 0)
            lo = by - H if off > 0 else 0
            dst = 0 if off > 0 else H + by
            res.append(
                remote(
                    ref.at[:, lo : lo + H],
                    ext.at[H : H + bx, dst : dst + H, :L],
                    send.at[k], recv.at[k], 1, off,
                )
            )
        return res

    def corner_copies(off):
        res = []
        for n, (ext, w) in enumerate(((ue, H), (be, H - 2))):
            for side in range(2):
                k = 8 + n * 4 + side * 2 + (off > 0)
                xs = H - w if side == 0 else H + bx
                lo = by if off > 0 else H
                dst = 0 if off > 0 else H + by
                res.append(
                    remote(
                        ext.at[xs : xs + w, lo : lo + H, :L],
                        ext.at[xs : xs + w, dst : dst + H, :L],
                        send.at[k], recv.at[k], 1, off,
                    )
                )
        return res

    both = (-1, 1)
    for off in both:
        start_if(0, off, x_copies(off))
    for off in both:
        start_if(1, off, y_copies(off))
    for off in both:
        recv_if(0, off, x_copies(off))
    for off in both:
        start_if(1, off, corner_copies(off))
    for off in both:
        recv_if(1, off, y_copies(off) + corner_copies(off))

    per = L // H
    lane = lax.broadcasted_iota(jnp.int32, (by + 2 * H, L), 1)
    groups = (bx + 2 * H) // per
    if nz > 1:
        for n, ext in enumerate((ue, be)):
            for g in range(groups):
                low = jnp.zeros((by + 2 * H, L), F32)
                high = jnp.zeros((by + 2 * H, L), F32)
                for k in range(per):
                    plane = ext[g * per + k, :, :L]
                    here = (lane // H) == k
                    low = jnp.where(here, pltpu.roll(plane, (k * H) % L, 1), low)
                    high = jnp.where(here, pltpu.roll(plane, ((k + 1) * H) % L, 1), high)
                packs[0, n, g] = low
                packs[1, n, g] = high

        def z_copies(off):
            k = int(off > 0)
            return [remote(packs.at[k], unpacks.at[k], zsend.at[k], zrecv.at[k], 2, off)]

        for off in both:
            start_if(2, off, z_copies(off))
        for off in both:
            recv_if(2, off, z_copies(off))
        for n, ext in enumerate((ue, be)):
            for g in range(groups):
                upper, lower = unpacks[0, n, g], unpacks[1, n, g]
                for k in range(per):
                    up = pltpu.roll(upper, (L - k * H) % L, 1)
                    lo = pltpu.roll(lower, (L - (k + 1) * H) % L, 1)
                    ext[g * per + k, :, L:] = jnp.where(
                        lane < H, up, jnp.where(lane >= L - H, lo, 0.0)
                    )

    def masks_and_diagonals(level, rows, lanes, y_first, y_end, z_of_lane, z_ok, z_first):
        yy = lax.broadcasted_iota(jnp.int32, (rows, lanes), 0)
        zz = lax.broadcasted_iota(jnp.int32, (rows, lanes), 1)
        y_even, z_even = yy % 2 == 0, zz % 2 == 0
        gy = y_first + yy
        gz = z_first + z_of_lane(zz)
        n_y, n_z = (ny * by) >> level, (nz * bz) >> level
        ok = (gy >= 0) & (gy < n_y) & (yy < y_end) & (gz >= 0) & (gz < n_z) & z_ok(zz)
        mask = jnp.where(ok, 1.0, 0.0)
        my = jnp.where(y_even, 8.0, 16.0) / 30.0
        mz = jnp.where(z_even, 8.0, 16.0) / 30.0
        ky = jnp.where(y_even, 14.0, 16.0) / 3.0
        kz = jnp.where(z_even, 14.0, 16.0) / 3.0
        inv = []
        for kx, mx in ((14.0 / 3.0, 8.0 / 30.0), (16.0 / 3.0, 16.0 / 30.0)):
            diag = 2.0**level * (kx * my * mz + mx * ky * mz + mx * my * kz)
            inv.append(mask / diag)
        return mask, inv

    def filter_planes(src, lines, acc, first, pairs):
        rows, lanes = src.shape[1], src.shape[2]

        def body(p, carry):
            x = first + 4 * p
            for k in range(4):
                m, w = z_filters(src[x + k])
                for lt in range(lanes // 128):
                    cut = slice(128 * lt, 128 * lt + 128)
                    lines[k, 0, lt, 8 : 8 + rows] = m[:, cut]
                    lines[k, 1, lt, 8 : 8 + rows] = w[:, cut]
                for lt in range(lanes // 128):
                    for t in range(rows // 16):

                        def rows_of(n, off):
                            return lines[k, n, lt, pl.ds(8 + 16 * t + off, 8, stride=2)]

                        me, mo, we, wo = (
                            rows_of(n, off) for n in range(2) for off in range(2)
                        )
                        next_me, next_we = rows_of(0, 2), rows_of(1, 2)
                        m_e = mo + rows_of(0, -1)
                        w_e = wo + rows_of(1, -1)
                        m_o = me + next_me
                        w_o = we + next_we
                        m_ee = rows_of(0, -2) + next_me
                        w_ee = rows_of(1, -2) + next_we
                        ev = pl.ds(16 * t, 8, stride=2)
                        od = pl.ds(16 * t + 1, 8, stride=2)
                        acc[0, x + k, lt, ev] = 8.0 * me + 2.0 * m_e - m_ee
                        acc[0, x + k, lt, od] = 16.0 * mo + 2.0 * m_o
                        acc[1, x + k, lt, ev] = (22.0 * me - 6.0 * m_e) + (
                            8.0 * we + 2.0 * w_e - w_ee
                        )
                        acc[1, x + k, lt, od] = (32.0 * mo - 6.0 * m_o) + (
                            16.0 * wo + 2.0 * w_o
                        )
            return carry

        lax.fori_loop(0, pl.cdiv(2 * pairs, 4), body, 0)

    def applied(acc, first, pairs, level, use):
        scale = 2.0**level / 2700.0

        def body(p, carry):
            x = first + 2 * p
            for t in range(acc.shape[3] // 8 - 1):
                for lt in range(acc.shape[2]):
                    y = slice(8 * t, 8 * t + 8)
                    a = [acc[0, x + k, lt, y] for k in range(-1, 3)]
                    c = [acc[1, x + k, lt, y] for k in range(-2, 4)]
                    even = (22.0 * a[1] - 6.0 * (a[0] + a[2])) + (
                        8.0 * c[2] + 2.0 * (c[1] + c[3]) - (c[0] + c[4])
                    )
                    odd = (32.0 * a[2] - 6.0 * (a[1] + a[3])) + (
                        16.0 * c[3] + 2.0 * (c[2] + c[4])
                    )
                    use(x, 0, scale * even, t, lt)
                    use(x + 1, 1, scale * odd, t, lt)
            return carry

        lax.fori_loop(0, pairs, body, 0)

    rows0, lanes0 = by + 2 * H, 2 * bz
    mask0, inv0 = masks_and_diagonals(
        0, rows0, lanes0, iy * by - H, rows0,
        lambda z: jnp.where(z < bz + bz // 2, z, z - 2 * bz), lambda z: z >= 0, iz * bz,
    )

    def x_mask(level, x, x_first):
        g = x_first + x
        return jnp.where((g >= 0) & (g < ((nx * bx) >> level)), 1.0, 0.0).astype(F32)

    gx0 = ix * bx - H

    def tile(t, lt):
        return (slice(8 * t, 8 * t + 8), slice(128 * lt, 128 * lt + 128))

    def use_residual(x, odd, av, t, lt):
        y = tile(t, lt)
        r = be[(x, *y)] - av
        r0[(x, *y)] = r
        d0[(x, *y)] = (inv0[odd][y] * (FIRST * x_mask(0, x, gx0))) * r

    filter_planes(ue, y0, a0, 0, (bx + 16) // 2)
    applied(a0, 2, (bx + 12) // 2, 0, use_residual)
    own0 = (slice(H, H + bx), slice(H, H + by), slice(0, bz))
    out_ref[...] = u_ref[...] + d0[own0]

    def use_step(x, odd, av, t, lt):
        y = tile(t, lt)
        r = r0[(x, *y)] - av
        r0[(x, *y)] = r
        d0[(x, *y)] = KEEP * d0[(x, *y)] + (inv0[odd][y] * (STEP * x_mask(0, x, gx0))) * r

    filter_planes(d0, y0, a0, 2, (bx + 12) // 2)
    applied(a0, 4, (bx + 8) // 2, 0, use_step)
    out_ref[...] += d0[own0]

    def use_down(x, odd, av, t, lt):
        y = tile(t, lt)
        r0[(x, *y)] = (r0[(x, *y)] - av) * (mask0[y] * x_mask(0, x, gx0))

    filter_planes(d0, y0, a0, 2, (bx + 10) // 2)
    applied(a0, 4, (bx + 6) // 2, 0, use_down)

    def narrowed(ref, x):
        even = (
            ref[x] + 0.375 * (ref[x - 1] + ref[x + 1]) - 0.125 * (ref[x - 3] + ref[x + 3])
        )
        odd = ref[x + 2] + 0.75 * (ref[x + 1] + ref[x + 3])
        return even, odd

    coarse = []
    for q in range(cx // 2):
        for plane in narrowed(r0, H + 4 * q):
            coarse.append(exact(ry0[...], plane))
    rhs = zdot(jnp.concatenate(coarse, axis=0), rz0[...])
    wl = cz + 2 * ZR
    blk[...] = rhs.reshape(cx, cy, wl)

    if nz > 1:

        def gz_copies(off):
            k = int(off > 0)
            return [remote(blk, zin.at[k], gzsend.at[k], gzrecv.at[k], 2, off)]

        for off in both:
            start_if(2, off, gz_copies(off))
        for off in both:
            recv_if(2, off, gz_copies(off))
        wlane = lax.broadcasted_iota(jnp.int32, (cy, wl), 1)
        for p in range(cx):
            lower = pltpu.roll(zin[1, p], wl - cz, 1)
            upper = pltpu.roll(zin[0, p], cz, 1)
            zin[2, p] = jnp.where(
                wlane < ZR, lower, jnp.where(wlane >= ZR + cz, upper, blk[p])
            )
    else:
        zin[2] = blk[...]

    def slot(axis, off):
        if (full_x, full_y)[axis]:
            return (ix, iy)[axis]
        return REACH - off

    def spot(axis, off, size):
        return pl.ds(pl.multiple_of(slot(axis, off) * size, size), size)

    def gx_copies(off):
        k = off + REACH * 2
        dst = g1.at[spot(0, off, cx), spot(1, 0, cy)]
        return [remote(zin.at[2], dst, gsend.at[0, k], grecv.at[0, k], 0, off)]

    def gy_copies(off):
        k = off + REACH * 2
        src = g1.at[:, spot(1, 0, cy)]
        dst = g1.at[:, spot(1, off, cy)]
        return [remote(src, dst, gsend.at[1, k], grecv.at[1, k], 1, off)]

    for off in offsets[0]:
        start_if(0, off, gx_copies(off))
    g1[spot(0, 0, cx), spot(1, 0, cy)] = zin[2]
    rows1, planes1 = g1.shape[1], cx * wx
    y1[...] = jnp.zeros_like(y1)
    y2[...] = jnp.zeros_like(y2)
    d1[...] = jnp.zeros_like(d1)
    a1[...] = jnp.zeros_like(a1)
    d2[...] = jnp.zeros_like(d2)
    a2[...] = jnp.zeros_like(a2)
    c1[...] = jnp.zeros_like(c1)
    r1[...] = jnp.zeros_like(r1)
    t2[...] = jnp.zeros_like(t2)
    for off in offsets[0]:
        recv_if(0, off, gx_copies(off))
    for off in offsets[1]:
        start_if(1, off, gy_copies(off))
    for off in offsets[1]:
        recv_if(1, off, gy_copies(off))

    Q = 8
    mask1, inv1 = masks_and_diagonals(
        1, rows1, wl, start_y * cy, cy * wy, lambda z: z, lambda z: z >= 0, iz * cz - ZR
    )
    gx1 = start_x * cx - Q

    def first_mid(p, carry):
        for odd in range(2):
            x = 2 * p + odd
            r = g1[x]
            r1[x + Q] = r
            d = (inv1[odd] * (FIRST * x_mask(1, x + Q, gx1))) * r
            d1[x + Q] = d
            s1[x] = d
        return carry

    lax.fori_loop(0, planes1 // 2, first_mid, 0)

    def use_step1(x, odd, av, t, lt):
        y = tile(t, lt)
        r = r1[(x, *y)] - av
        r1[(x, *y)] = r
        d = KEEP * d1[(x, *y)] + (inv1[odd][y] * (STEP * x_mask(1, x, gx1))) * r
        d1[(x, *y)] = d
        s1[(x - Q, *y)] += d

    def use_down1(x, odd, av, t, lt):
        y = tile(t, lt)
        r1[(x, *y)] = (r1[(x, *y)] - av) * (mask1[y] * x_mask(1, x, gx1))

    half1 = planes1 // 2
    filter_planes(d1, y1, a1, Q, half1)
    applied(a1, Q, half1, 1, use_step1)
    filter_planes(d1, y1, a1, Q, half1)
    applied(a1, Q, half1, 1, use_down1)

    planes2 = planes1 // 2
    rows2 = d2.shape[1]
    mask2, inv2 = masks_and_diagonals(
        2, rows2, wl, start_y * (cy // 2), cy * wy // 2, lambda z: z,
        lambda z: z < wl // 2, iz * (cz // 2) - ZR // 2,
    )
    gx2 = start_x * (cx // 2) - Q

    def down_mid(q, carry):
        parts = [exact(ry1[...], plane) for plane in narrowed(r1, Q + 4 * q)]
        prod = zdot(jnp.concatenate(parts, axis=0), rz1[...])
        for odd in range(2):
            x = 2 * q + odd + Q
            r = prod[odd * rows2 : (odd + 1) * rows2]
            r2[x] = r
            d2[x] = (inv2[odd] * (FIRST * x_mask(2, x, gx2))) * r
        return carry

    lax.fori_loop(0, planes2 // 2, down_mid, 0)
    filter_planes(d2, y2, a2, Q, planes2 // 2)

    def use_last(x, odd, av, t, lt):
        y = tile(t, lt)
        r = r2[(x, *y)] - av
        step = (inv2[odd][y] * (STEP * x_mask(2, x, gx2))) * r
        d2[(x, *y)] = (1.0 + KEEP) * d2[(x, *y)] + step

    applied(a2, Q, planes2 // 2, 2, use_last)

    def up_last(p, carry):
        v = zdot(d2[pl.ds(Q + 2 * p, 2)].reshape(2 * rows2, wl), pz1[...])
        for k in range(2):
            t2[2 * p + k] = exact(py1[...], v[k * rows2 : (k + 1) * rows2])
        return carry

    lax.fori_loop(0, planes2 // 2, up_last, 0)

    def widened(ref, x):
        one, two, three = ref[x], ref[x + 1], ref[x + 2]
        return (
            one,
            0.375 * one + 0.75 * two - 0.125 * three,
            two,
            -0.125 * one + 0.75 * two + 0.375 * three,
        )

    def up_mid(q, carry):
        for k, plane in enumerate(widened(t2, 2 * q)):
            x = 4 * q + k
            e = plane * (mask1 * x_mask(1, x + Q, gx1))
            d1[x + Q] = e
            s1[x] += e
        return carry

    lax.fori_loop(0, planes1 // 4, up_mid, 0)
    filter_planes(d1, y1, a1, Q, half1)

    def use_up1(x, odd, av, t, lt):
        y = tile(t, lt)
        r = r1[(x, *y)] - av
        r1[(x, *y)] = r
        d = (inv1[odd][y] * (FIRST * x_mask(1, x, gx1))) * r
        d1[(x, *y)] = d
        s1[(x - Q, *y)] += d

    applied(a1, Q, half1, 1, use_up1)
    filter_planes(d1, y1, a1, Q, half1)

    def use_final1(x, odd, av, t, lt):
        y = tile(t, lt)
        r = r1[(x, *y)] - av
        d = KEEP * d1[(x, *y)] + (inv1[odd][y] * (STEP * x_mask(1, x, gx1))) * r
        c1[(x, *tile(t + 1, lt))] = s1[(x - Q, *y)] + d

    applied(a1, Q, half1, 1, use_final1)

    crow = cy + 16
    own_x = (ix if full_x else REACH) * cx + Q
    own_y = pl.multiple_of((iy if full_y else REACH) * cy, 8)

    def up_first(p, carry):
        x = own_x - 2 + 2 * p
        v = c1[pl.ds(x, 2), pl.ds(own_y, crow)].reshape(2 * crow, wl)
        v = zdot(v, pz0[...])
        for k in range(2):
            c0[2 * p + k] = exact(py0[...], v[k * crow : (k + 1) * crow])
        return carry

    lax.fori_loop(0, (cx + 6) // 2, up_first, 0)

    def up_fine(q, carry):
        for k, plane in enumerate(widened(c0, 2 * q)):
            x = H - 4 + 4 * q + k
            d0[x] = plane * (mask0 * x_mask(0, x, gx0))
        return carry

    lax.fori_loop(0, (bx + 8) // 4, up_fine, 0)
    out_ref[...] += d0[own0]
    filter_planes(d0, y0, a0, 4, (bx + 8) // 2)

    def use_up(x, odd, av, t, lt):
        y = tile(t, lt)
        r = r0[(x, *y)] - av
        r0[(x, *y)] = r
        d0[(x, *y)] = (inv0[odd][y] * (FIRST * x_mask(0, x, gx0))) * r

    applied(a0, 6, (bx + 4) // 2, 0, use_up)
    filter_planes(d0, y0, a0, 6, (bx + 4) // 2)

    def use_final(x, odd, av, t, lt):
        if t == 0 or t == by // 8 + 1 or lt >= bz // 128:
            return
        y = tile(t, lt)
        r = r0[(x, *y)] - av
        d = d0[(x, *y)]
        new = d + (KEEP * d + (inv0[odd][y] * STEP) * r)
        out_ref[(x - H, *tile(t - 1, lt))] += new

    applied(a0, H, bx // 2, 0, use_final)

    for off in both:
        sent_if(0, off, x_copies(off))
        sent_if(1, off, y_copies(off) + corner_copies(off))
        if nz > 1:
            sent_if(2, off, z_copies(off) + gz_copies(off))
    for off in offsets[0]:
        sent_if(0, off, gx_copies(off))
    for off in offsets[1]:
        sent_if(1, off, gy_copies(off))


def local(mesh_shape, u, b):
    nx, ny, nz = (mesh_shape[a] for a in ("gx", "gy", "gz"))
    bx, by, bz = u.shape
    cx, cy, cz = bx // 2, by // 2, bz // 2
    wx = nx if nx <= 2 * REACH + 1 else 2 * REACH + 1
    wy = ny if ny <= 2 * REACH + 1 else 2 * REACH + 1
    wl = cz + 2 * ZR
    rows0, lanes0 = by + 2 * H, 2 * bz
    rows1, planes1 = -(-cy * wy // 16) * 16, cx * wx
    rows2, planes2 = -(-cy * wy // 32) * 16, planes1 // 2
    crow = cy + 16

    def z_pos(z):
        return z if z >= 0 else z + lanes0

    rz0 = transfer(restrict_taps, range(cz), lambda o: o + ZR, z_pos, wl, lanes0, 2).T
    ry0 = transfer(restrict_taps, range(cy), lambda o: o, lambda f: f + H, cy, rows0, 2)
    rz1 = transfer(restrict_taps, range(wl // 2), lambda o: o, lambda f: f, wl, wl, 2).T
    live1 = lambda f: f if 0 <= f < cy * wy else None
    ry1 = transfer(restrict_taps, range(cy * wy // 2), lambda o: o, live1, rows2, rows1, 2)
    pz1 = transfer(prolong_taps, range(wl), lambda o: o, lambda c: c, wl, wl, 0).T
    live2 = lambda c: c if 0 <= c < cy * wy // 2 else None
    py1 = transfer(prolong_taps, range(cy * wy), lambda o: o, live2, rows1, rows2, 0)
    pz0 = transfer(
        prolong_taps, range(-H, bz + H), z_pos, lambda c: c + ZR, lanes0, wl, 0
    ).T
    py0 = transfer(
        prolong_taps, range(-H, by + H), lambda o: o + H, lambda c: c + 8, rows0, crow, 0
    )
    bf = lambda m: jnp.asarray(m, BF16)
    fl = lambda m: jnp.asarray(m, F32)
    consts = (
        bf(rz0), fl(ry0), bf(rz1), fl(ry1), bf(pz1), fl(py1),
        bf(pz0), fl(py0),
    )
    vm = lambda *s: pltpu.VMEM(s, F32)
    groups = (bx + 2 * H) // (bz // H)
    dma = lambda *s: pltpu.SemaphoreType.DMA(s)
    geo = (nx, ny, nz, bx, by, bz, wx, wy)
    return pl.pallas_call(
        functools.partial(kernel, geo),
        out_shape=jax.ShapeDtypeStruct(u.shape, F32),
        in_specs=[pl.BlockSpec(memory_space=pltpu.VMEM)] * (2 + len(consts)),
        out_specs=pl.BlockSpec(memory_space=pltpu.VMEM),
        scratch_shapes=[
            vm(bx + 16, rows0, lanes0), vm(bx + 16, rows0, lanes0),
            vm(bx + 16, rows0, lanes0), vm(bx + 16, rows0, lanes0),
            vm(2, bx + 16, lanes0 // 128, rows0 + 8, 128), vm(cx + 8, rows0, lanes0),
            vm(2, 2, groups, rows0, bz), vm(2, 2, groups, rows0, bz),
            vm(4, 2, lanes0 // 128, rows0 + 16, 128), vm(4, 2, wl // 128, rows1 + 16, 128),
            vm(4, 2, wl // 128, rows2 + 16, 128), vm(cx, cy, wl), vm(3, cx, cy, wl),
            vm(planes1, rows1, wl), vm(planes1 + 16, rows1, wl),
            vm(planes1 + 16, rows1, wl), vm(planes1, rows1, wl),
            vm(2, planes1 + 16, wl // 128, rows1 + 8, 128), vm(planes1 + 16, rows1 + 16, wl),
            vm(planes2 + 16, rows2, wl), vm(planes2 + 16, rows2, wl),
            vm(2, planes2 + 16, wl // 128, rows2 + 8, 128), vm(planes2 + 8, rows1, wl),
            dma(16), dma(16), dma(2), dma(2),
            dma(2, 4 * REACH + 1), dma(2, 4 * REACH + 1), dma(2), dma(2),
        ],
        compiler_params=pltpu.CompilerParams(
            collective_id=0, has_side_effects=True, vmem_limit_bytes=60 * 1024 * 1024
        ),
    )(u, b, *consts)


def solution(mesh):
    placed = P("gx", "gy", "gz")
    return jax.shard_map(
        functools.partial(local, dict(mesh.shape)), mesh=mesh,
        in_specs=(placed, placed), out_specs=placed, check_vma=False,
    )
```

profile of v0, /device:TPU:0, one launch (start us, length us, event | category | flops | bytes accessed | tf_op | source)
XLA Modules:
  0.0 57.7 jit_solution(11429408941095982838)
XLA Ops:
  0.0 56.1 %shard_map.100 = f32[16,16,128]{2,1,0:T(8,128)} custom-call(f32[16,16,128]{2,1,0:T(8,128)} %u_ref.1, f32[16,16,128]{2,1,0:T(8,128)} %b_ref.1, bf16[256,128]{1,0:T(8,128)(2,1)} %constant.16.clone.rz0, f32[8,32]{1,0:T(8,128)} %constant.17.clone.ry0, bf16[128,128]{1,0:T(8,128)(2,1)} %constant.18.clone.rz1, f32[16,32]{1,0:T(8,128)} %constant.19.clone.ry1, ...), custom_call_target="tpu_custom_call" | custom-call | tf_op jit(solution)/shard_map/pallas_call | solution.py:649
  56.1 1.6 %copy.12 = f32[16,16,128]{2,1,0:T(8,128)} copy(f32[16,16,128]{2,1,0:T(8,128)} %shard_map.100) | data formatting | bytes 262144
where the time goes:
time: 58.6 us; the launch traced here: 57.7 us
  Pallas kernels  56.1 us (96%)
  local copies, waits for them, and re-layouts  1.57 us (3%)
    pallas_call x1, Pallas kernels, local(): pl.pallas_call(functools.partial(kernel, geo), out_shape=jax.ShapeDtypeSt...  56.1 us
    unnamed x1, local copies, waits for them, and re-layouts  1.57 us

commit v1 on v0

v1 whole, which is shorter than its diff:
```python
import functools

import jax
import jax.numpy as jnp
import numpy as np
from jax import lax
from jax.experimental import pallas as pl
from jax.experimental.pallas import tpu as pltpu
from jax.sharding import PartitionSpec as P

F32 = jnp.float32
BF16 = jnp.bfloat16
MESH = pl.DeviceIdType.MESH
H = 8
ZR = 32
REACH = 3
LANES = 128

RHO0 = 1.0 / 1.2
RHO1 = 1.0 / (2.4 - RHO0)
FIRST = 1.0 / 1.32
KEEP = RHO1 * RHO0
STEP = 2.0 * RHO1 / 1.1
RATIO = STEP / FIRST
UNIT = 2700.0


def restrict_taps(g):
    if g % 2 == 0:
        return ((-3, -0.125), (-1, 0.375), (0, 1.0), (1, 0.375), (3, -0.125))
    return ((-1, 0.75), (0, 1.0), (1, 0.75))


def prolong_taps(f):
    if f % 2 == 0:
        return ((f // 2, 1.0),)
    q = f // 4
    if f % 4 == 1:
        return ((2 * q, 0.375), (2 * q + 1, 0.75), (2 * q + 2, -0.125))
    return ((2 * q, -0.125), (2 * q + 1, 0.75), (2 * q + 2, 0.375))


def stiff_taps(i):
    if i % 2 == 0:
        return {-2: 1, -1: -8, 0: 14, 1: -8, 2: 1}
    return {-1: -8, 0: 16, 1: -8}


def mass_taps(i):
    if i % 2 == 0:
        return {-2: -1, -1: 2, 0: 8, 1: 2, 2: -1}
    return {-1: 2, 0: 16, 1: 2}


class Level:
    def __init__(self, group, tiles, height, half, at, parts):
        self.group, self.tiles, self.height, self.half, self.at = group, tiles, height, half, at
        self.parts = parts
        self.rows = 2 * half
        self.paired = group >= 4


def operator_matrix(lv):
    k = 256 if lv.paired else 384
    m = np.zeros((k, 256), np.float64)
    for x in range(lv.group):
        for y in range(lv.height):
            for ox, mx in mass_taps(x).items():
                kx = stiff_taps(x)[ox]
                p = x + ox
                if lv.paired:
                    block = (p + lv.group // 2) // lv.group
                else:
                    block = p // lv.group + 1
                for oy, my in mass_taps(y).items():
                    ky = stiff_taps(y)[oy]
                    if not 0 <= y + oy < lv.height:
                        continue
                    row = block * LANES + lv.at(p % lv.group, y + oy)
                    both, mixed = mx * my, kx * my + mx * ky
                    m[row, lv.at(x, y)] = -8 * both + 2 * mixed
                    m[row, LANES + lv.at(x, y)] = both - mixed
    return m


def plane_matrix(n_in, n_out, pairs_x, pairs_y, at_in, at_out):
    m = np.zeros((n_in * LANES, n_out * LANES), np.float64)
    for (to, xo), ti, xi, wx in pairs_x:
        for yo, yi, wy in pairs_y:
            m[ti * LANES + at_in(xi, yi), to * LANES + at_out(xo, yo)] += wx * wy
    return m


def to_bf16(m):
    out = jnp.asarray(m, BF16)
    assert np.array_equal(np.asarray(m, jnp.bfloat16).astype(np.float64), m)
    return out


def split(v):
    hi = v.astype(BF16)
    return hi, (v - hi.astype(F32)).astype(BF16)


def loop(count, body, most=9):
    if count <= most:
        for i in range(count):
            body(i)
    else:

        def step(i, carry):
            body(i)
            return carry

        lax.fori_loop(0, count, step, 0)


def kernel(
    geo, lv0, lv1, lv2, offs, u_ref, b_ref, *refs,
):
    (wa0_h, wa1_h, wa2_h, wr0_h, wr1_h, wp1_h, wp0_h, out_ref,
     wa0, wa1, wa2, wr0, wr1, wp1, wp0,
     ue, be, tmp, strip_out, strip_in,
     d0, r0, acc0, hh0, hl0, ss0, iv0, mk0, zm0,
     d1, r1, acc1, hh1, hl1, ss1, iv1, mk1, zm1, c1,
     d2, r2, hh2, hl2, ss2, iv2, mk2, zm2,
     xs0, xs1, blk, line, land, up2, zp1, zp0, zh1, zl1, zh0, zl0,
     wsem, xysend, xyrecv, zsend, zrecv, gsend, grecv, psend, precv) = refs
    nx, ny, nz, bx, by, bz, wx, wy, wyp = geo
    ix, iy, iz = lax.axis_index("gx"), lax.axis_index("gy"), lax.axis_index("gz")
    place, counts = (ix, iy, iz), (nx, ny, nz)
    full_x, full_y = wx == nx, wy == ny
    cx, cy, cz = bx // 2, by // 2, bz // 2
    start_x = 0 if full_x else ix - REACH
    start_y = 0 if full_y else iy - REACH
    own_x = ix if full_x else REACH
    own_y = iy if full_y else REACH
    offs_xy, offs_z, offs_g, offs_p = offs

    def there(off, sign=1):
        ok = None
        for p, n, o in zip(place, counts, off):
            if o:
                q = p + sign * o
                c = (q >= 0) & (q < n)
                ok = c if ok is None else ok & c
        return ok

    def device(off):
        return tuple(p + o for p, o in zip(place, off))

    barrier = pltpu.get_barrier_semaphore()
    total = 0
    for off in sorted(set(offs_xy + offs_z + offs_g + offs_p)):
        ok = there(off)
        total = total + ok.astype(jnp.int32)

        @pl.when(ok)
        def _():
            pl.semaphore_signal(
                barrier, inc=1, device_id=device(off), device_id_type=MESH
            )

    loads = [
        pltpu.make_async_copy(s, d, wsem.at[n])
        for n, (s, d) in enumerate(
            ((wa0_h, wa0), (wr0_h, wr0), (wa1_h, wa1), (wr1_h, wr1), (wa2_h, wa2),
             (wp1_h, wp1), (wp0_h, wp0))
        )
    ]
    for c in loads:
        c.start()

    def remote(src, dst, ss, rs, off):
        return pltpu.make_async_remote_copy(
            src_ref=src, dst_ref=dst, send_sem=ss, recv_sem=rs,
            device_id=device(off), device_id_type=MESH,
        )

    def start_if(off, copies):
        @pl.when(there(off))
        def _():
            for c in copies:
                c.start()

    def recv_if(off, copies):
        @pl.when(there(off, -1))
        def _():
            for c in copies:
                c.wait_recv()

    def sent_if(off, copies):
        @pl.when(there(off))
        def _():
            for c in copies:
                c.wait_send()

    def cut(off, size, low, high):
        if off == 0:
            return slice(0, size), slice(H, H + size)
        if off > 0:
            return slice(size - low, size), slice(H - low, H)
        return slice(0, high), slice(H + size, H + size + high)

    fields = ((u_ref, ue, H, H - 1), (b_ref, be, H - 2, H - 3))

    def halo_cut(off, k):
        ref, ext, low, high = fields[k]
        sx, tx = cut(off[0], bx, low, high)
        sy, ty = cut(off[1], by, H, H)
        return ref, ext, sx, tx, sy, ty

    def zero(ref, *at):
        ref[at] = jnp.zeros_like(ref[at])

    def halo_copies(n, which=(0, 1)):
        off = offs_xy[n]
        res = []
        for k in which:
            ref, ext, sx, tx, sy, ty = halo_cut(off, k)
            res.append(
                remote(
                    ref.at[sx, sy], ext.at[tx, ty], xysend.at[n, k], xyrecv.at[n, k], off
                )
            )
        return res

    pl.semaphore_wait(barrier, total)
    for n, off in enumerate(offs_xy):
        start_if(off, halo_copies(n, (0,)))
    for n, off in enumerate(offs_xy):
        start_if(off, halo_copies(n, (1,)))

    ue[H : H + bx, H : H + by] = u_ref[...]
    be[H : H + bx, H : H + by] = b_ref[...]
    for _, ext, low, high in fields:
        for at in (slice(0, H - low), slice(H + bx + high, 2 * H + bx)):
            if at.stop > at.start:
                zero(ext, at)
    for off in [(a, c, 0) for a in (-1, 0, 1) for c in (-1, 0, 1) if a or c]:

        def clear():
            for k in range(2):
                _, ext, _, tx, _, ty = halo_cut(off, k)
                zero(ext, tx, ty)

        if off in offs_xy:
            pl.when(jnp.logical_not(there(off, -1)))(clear)
        else:
            clear()
    zq, half_c = ZR // 2, cz // 2
    for side, rows in ((-1, slice(zq + half_c, 2 * zq + half_c)), (1, slice(0, zq))):

        def clear():
            zero(strip_in, (side + 1) // 2)
            zero(land, slice(None), slice(None), rows)

        if nz > 1:
            pl.when(jnp.logical_not(there((0, 0, side), -1)))(clear)
        else:
            clear()
    if not full_x:
        for off in offs_g:

            @pl.when(jnp.logical_not(there(off, -1)))
            def _():
                zero(line, REACH - off[0])

    if not full_y:
        for off in offs_p:
            if off[2] == 0:

                @pl.when(jnp.logical_not(there(off, -1)))
                def _():
                    zero(land, REACH - off[1])


    def set_up(lv, level, iv, mk, zm, d, ss, x_first, y_first, z_first, x_at, y_at):
        lane = lax.broadcasted_iota(jnp.int32, (8, LANES), 1)
        row = lax.broadcasted_iota(jnp.int32, (lv.half, LANES), 0)
        xx, yy = x_at(lane), y_at(lane)
        x_even, y_even = xx % 2 == 0, yy % 2 == 0
        n_x, n_y, n_z = (nx * bx) >> level, (ny * by) >> level, (nz * bz) >> level
        gy = y_first + yy
        y_ok = (gy >= 0) & (gy < n_y) & (yy < lv.height)
        mass = lambda e: jnp.where(e, 8.0, 16.0) / 30.0
        stiff = lambda e: jnp.where(e, 14.0, 16.0) / 3.0
        my, ky, mx, kx = mass(y_even), stiff(y_even), mass(x_even), stiff(x_even)
        inv = []
        for kz, mz in ((14.0 / 3.0, 8.0 / 30.0), (16.0 / 3.0, 16.0 / 30.0)):
            inv.append((FIRST / UNIT) / (kx * my * mz + mx * ky * mz + mx * my * kz))

        def one(t):
            gx = x_first + t * lv.group + xx
            ok = jnp.where(y_ok & (gx >= 0) & (gx < n_x), 1.0, 0.0).astype(F32)
            mk[t] = ok
            iv[t, 0] = inv[0] * ok
            iv[t, 1] = inv[1] * ok

        loop(lv.tiles, one)
        for par in range(2):
            gz = z_first + 2 * row + par
            zm[par] = jnp.where((gz >= 0) & (gz < n_z), 1.0, 0.0).astype(F32)
        d[0] = jnp.zeros_like(d[0])
        d[lv.tiles + 1] = jnp.zeros_like(d[0])
        ss[:, :, 0:8] = jnp.zeros_like(ss[:, :, 0:8])
        ss[:, :, 8 + lv.half :] = jnp.zeros_like(ss[:, :, 8 + lv.half :])

    gs = LANES // wyp
    yh0 = by + 2 * H
    set_up(
        lv0, 0, iv0, mk0, zm0, d0, ss0, ix * bx - H, iy * by - H, iz * bz - H,
        lambda n: n // yh0, lambda n: n % yh0,
    )
    set_up(
        lv1, 1, iv1, mk1, zm1, d1, ss1, start_x * cx, start_y * cy, iz * cz - ZR,
        lambda n: (n % gs) // cy, lambda n: (n // gs) * cy + n % cy,
    )
    yh2 = LANES // lv2.group
    set_up(
        lv2, 2, iv2, mk2, zm2, d2, ss2, start_x * (cx // 2), start_y * (cy // 2),
        iz * (cz // 2) - ZR // 2, lambda n: n // yh2, lambda n: n % yh2,
    )
    c1[0:2] = jnp.zeros_like(c1[0:2])
    c1[lv1.tiles + 2 :] = jnp.zeros_like(c1[0:2])
    xs1[:, 0:8] = jnp.zeros_like(xs1[:, 0:8])
    xs1[:, 8 + lv1.half :] = jnp.zeros_like(xs1[:, 8 + lv1.half :])
    up2[...] = jnp.zeros_like(up2)

    zh = H // 2
    hb = bz // 2

    def turned(ext, t):
        tmp[...] = ext[lv0.group * t : lv0.group * t + lv0.group].reshape(LANES, bz).T
        return tmp[pl.ds(0, hb, stride=2)], tmp[pl.ds(1, hb, stride=2)]

    def strips(n, t, par, val):
        lo, hi = par * zh, par * zh + zh
        strip_out[0, n, t, lo:hi] = val[:zh]
        strip_out[1, n, t, lo:hi] = val[hb - zh :]

    def z_copies(n):
        off = offs_z[n]
        k = 1 if off[2] > 0 else 0
        return [remote(strip_out.at[k], strip_in.at[k], zsend.at[k], zrecv.at[k], off)]

    for k, ext in enumerate((ue, be)):
        for n, off in enumerate(offs_xy):
            recv_if(off, halo_copies(n, (k,)))
        for t in range(lv0.tiles):
            for par, val in enumerate(turned(ext, t)):
                lo = par * lv0.half + zh
                strips(k, t, par, val)
                if k == 0:
                    d0[t + 1, lo : lo + hb] = val
                else:
                    r0[t, lo : lo + hb] = UNIT * val
    for n, off in enumerate(offs_z):
        start_if(off, z_copies(n))
    for n, off in enumerate(offs_z):
        recv_if(off, z_copies(n))
    for t in range(lv0.tiles):
        for par in range(2):
            for side in range(2):
                lo = par * lv0.half + (0 if side else zh + hb)
                rows = slice(lo, lo + zh)
                d0[t + 1, rows] = strip_in[side, 0, t, par * zh : par * zh + zh]
                r0[t, rows] = UNIT * strip_in[side, 1, t, par * zh : par * zh + zh]

    def stage(lv, d, hh, hl, lo, count):
        step = 48 if lv.rows % 48 == 0 else min(lv.rows, 64)
        lane = lax.broadcasted_iota(jnp.int32, (step, LANES), 1)
        if lv is lv1:
            plane = (lane % gs) // cy
        else:
            plane = lane // (LANES // lv.group)
        low = plane < lv.group // 2

        def one(i):
            t = lo + i
            for s in range(0, lv.rows, step):
                rows = slice(s, s + step)
                if lv.paired:
                    v = jnp.where(low, d[t + 1, rows], d[t, rows])
                else:
                    v = d[t, rows]
                hh[t, rows], hl[t, rows] = split(v)

        loop(count + (1 if lv.paired else 2), one)

    def sweep(lv, hh, hl, w, ss, zm, lo, count, use):
        chunk = 24 if lv.half % 24 == 0 else 32
        n_cat = 2 if lv.paired else 3
        size = 2 if count % 2 == 0 else 1

        def group(i):
            t0 = lo + size * i

            def lhs(h):
                return jnp.concatenate(
                    [h[pl.ds(t0 + j, size)].reshape(size * lv.rows, LANES) for j in range(n_cat)],
                    axis=1,
                )

            s = jnp.dot(lhs(hh), w[...], preferred_element_type=F32) + jnp.dot(
                lhs(hl), w[...], preferred_element_type=F32
            )
            for k in range(size):
                slot = (i % 2) * 2 + k if isinstance(i, int) else k
                for par in range(2):
                    at = k * lv.rows + par * lv.half
                    for c in range(2):
                        ss[slot, 2 * c + par, 8 : 8 + lv.half] = s[
                            at : at + lv.half, LANES * c : LANES * c + LANES
                        ]
                t = t0 + k
                for at in range(0, lv.half, chunk):

                    def rows_of(n, shift=0):
                        return ss[slot, n, pl.ds(8 + at + shift, chunk)]

                    even = (
                        (-11.0 / 3.0) * rows_of(0) + (-46.0 / 3.0) * rows_of(2)
                    ) + ((rows_of(1) + rows_of(1, -1)) + (rows_of(2, -1) + rows_of(2, 1)))
                    odd = ((-16.0 / 3.0) * rows_of(1) + (-80.0 / 3.0) * rows_of(3)) + (
                        rows_of(0) + rows_of(0, 1)
                    )
                    for par, val in enumerate((even, odd)):
                        edge = None
                        if at < lv.parts or at + chunk > lv.half - lv.parts:
                            edge = zm[par, at : at + chunk]
                        use(t, par, slice(par * lv.half + at, par * lv.half + at + chunk), val, edge)

        loop(count // size, group, 4)

    def wide(v, n):
        return jnp.broadcast_to(v[0:1], (n, LANES))

    def masked(v, edge):
        return v if edge is None else v * edge

    def n_rows(rows):
        return rows.stop - rows.start

    own_lo = H // lv0.group
    own_n = bx // lv0.group

    def own(t):
        return own_lo <= t < own_lo + own_n

    def reach(below, above):
        lo = (H - below) // lv0.group
        hi = (H + bx - 1 + above) // lv0.group
        return lo, hi - lo + 1

    def use_residual(t, par, rows, av, edge):
        r = r0[t, rows] - av
        r0[t, rows] = r
        d = masked(wide(iv0[t, par], n_rows(rows)) * r, edge)
        if own(t):
            acc0[t - own_lo, rows] = d0[t + 1, rows] + d
        d0[t + 1, rows] = d

    def use_step(t, par, rows, av, edge):
        r = r0[t, rows] - av
        r0[t, rows] = r
        d = KEEP * d0[t + 1, rows] + masked(
            (RATIO * wide(iv0[t, par], n_rows(rows))) * r, edge
        )
        if own(t):
            acc0[t - own_lo, rows] += d
        d0[t + 1, rows] = d

    def use_down(t, par, rows, av, edge):
        r0[t, rows] = masked((r0[t, rows] - av) * wide(mk0[t], n_rows(rows)), edge)

    lo_a, n_a = reach(6, 5)
    lo_b, n_b = reach(4, 3)
    loads[0].wait()
    stage(lv0, d0, hh0, hl0, lo_a, n_a)
    sweep(lv0, hh0, hl0, wa0, ss0, zm0, lo_a, n_a, use_residual)
    stage(lv0, d0, hh0, hl0, lo_b, n_b)
    sweep(lv0, hh0, hl0, wa0, ss0, zm0, lo_b, n_b, use_step)
    stage(lv0, d0, hh0, hl0, lo_b, n_b)
    sweep(lv0, hh0, hl0, wa0, ss0, zm0, lo_b, n_b, use_down)

    def restricted(parts, w):
        hi, lo = zip(*[split(p) for p in parts])
        return jnp.dot(
            jnp.concatenate(hi, axis=1), w, preferred_element_type=F32
        ) + jnp.dot(jnp.concatenate(lo, axis=1), w, preferred_element_type=F32)

    loads[1].wait()
    x = restricted([r0[lo_b + i] for i in range(n_b)], wr0[...])
    xs0[0] = x[: lv0.half]
    xs0[1] = x[lv0.half :]
    def pick(ref, par, start, n):
        return ref[par, pl.ds(start, n, stride=2)]

    def z_restricted(ref, even0, odd0, n):
        even = (
            0.5 * pick(ref, 0, even0, n)
            + 0.1875 * (pick(ref, 1, odd0, n) + pick(ref, 1, odd0 + 1, n))
            - 0.0625 * (pick(ref, 1, odd0 - 1, n) + pick(ref, 1, odd0 + 2, n))
        )
        odd = 0.5 * pick(ref, 0, even0 + 1, n) + 0.375 * (
            pick(ref, 1, odd0 + 1, n) + pick(ref, 1, odd0 + 2, n)
        )
        return even, odd

    even, odd = z_restricted(xs0, zh, zh - 1, half_c)
    lane_c = lax.broadcasted_iota(jnp.int32, (half_c, LANES), 1)
    packed = jnp.where(lane_c < LANES // 2, even, odd)
    blk[...] = packed

    def slot(axis, off):
        if (full_x, full_y)[axis]:
            return (ix, iy)[axis]
        return REACH - off

    def g_copies(n):
        off = offs_g[n]
        return [remote(blk, line.at[slot(0, off[0])], gsend.at[n], grecv.at[n], off)]

    def p_copies(n):
        off = offs_p[n]
        if off[2] == 0:
            src, dst = slice(0, half_c), slice(zq, zq + half_c)
        elif off[2] > 0:
            src, dst = slice(half_c - zq, half_c), slice(0, zq)
        else:
            src, dst = slice(0, zq), slice(zq + half_c, 2 * zq + half_c)
        return [
            remote(
                line.at[:, src], land.at[slot(1, off[1]), :, dst], psend.at[n], precv.at[n], off
            )
        ]

    for n, off in enumerate(offs_g):
        start_if(off, g_copies(n))
    line[own_x] = packed
    for n, off in enumerate(offs_g):
        recv_if(off, g_copies(n))
    for n, off in enumerate(offs_p):
        start_if(off, p_copies(n))
    land[own_y, :, zq : zq + half_c] = line[...]
    for n, off in enumerate(offs_p):
        recv_if(off, p_copies(n))

    per = cx // lv1.group
    lane_h = lax.broadcasted_iota(jnp.int32, (lv1.half, LANES), 1) // gs

    def place_block(jx):
        blocks = [land[jy, jx] for jy in range(wy)]
        for s in range(per):
            t = jx * per + s
            for par in range(2):
                at = par * (LANES // 2) + s * gs
                val = None
                for jy in range(wy):
                    shift = (jy * gs - at) % LANES
                    v = pltpu.roll(blocks[jy], shift, 1) if shift else blocks[jy]
                    if val is None:
                        val = v if wy == wyp else jnp.where(lane_h == jy, v, 0.0)
                    else:
                        val = jnp.where(lane_h == jy, v, val)
                rows = slice(par * lv1.half, par * lv1.half + lv1.half)
                r1[t, rows] = val
                d = (wide(iv1[t, par], lv1.half) * zm1[par]) * val
                d1[t + 1, rows] = d
                acc1[t, rows] = d

    loop(wx, place_block, 4)

    def use_step1(t, par, rows, av, edge):
        r = r1[t, rows] - av
        r1[t, rows] = r
        d = KEEP * d1[t + 1, rows] + masked(
            (RATIO * wide(iv1[t, par], n_rows(rows))) * r, edge
        )
        d1[t + 1, rows] = d
        acc1[t, rows] += d

    def use_down1(t, par, rows, av, edge):
        r1[t, rows] = masked((r1[t, rows] - av) * wide(mk1[t], n_rows(rows)), edge)

    loads[2].wait()
    n1 = lv1.tiles
    stage(lv1, d1, hh1, hl1, 0, n1)
    sweep(lv1, hh1, hl1, wa1, ss1, zm1, 0, n1, use_step1)
    stage(lv1, d1, hh1, hl1, 0, n1)
    sweep(lv1, hh1, hl1, wa1, ss1, zm1, 0, n1, use_down1)

    ratio = 2 * lv2.group // lv1.group
    r_lo = (-3) // lv1.group
    r_hi = (2 * lv2.group + 1) // lv1.group
    loads[3].wait()
    for t in range(lv2.tiles):
        a, e = max(0, ratio * t + r_lo), min(n1 - 1, ratio * t + r_hi)
        skip = (a - (ratio * t + r_lo)) * LANES
        x = restricted(
            [r1[i] for i in range(a, e + 1)], wr1[skip : skip + (e + 1 - a) * LANES]
        )
        xs1[0, 8 : 8 + lv1.half] = x[: lv1.half]
        xs1[1, 8 : 8 + lv1.half] = x[lv1.half :]
        for par, val in enumerate(z_restricted(xs1, 8, 7, lv2.half)):
            rows = slice(par * lv2.half, par * lv2.half + lv2.half)
            r2[t, rows] = val
            d2[t + 1, rows] = (wide(iv2[t, par], lv2.half) * zm2[par]) * val

    def use_last(t, par, rows, av, edge):
        r = r2[t, rows] - av
        step = masked((RATIO * wide(iv2[t, par], n_rows(rows))) * r, edge)
        lo = rows.start - par * lv2.half
        up2[t, par, lo : lo + n_rows(rows)] = (1.0 + KEEP) * d2[t + 1, rows] + step

    loads[4].wait()
    stage(lv2, d2, hh2, hl2, 0, lv2.tiles)
    sweep(lv2, hh2, hl2, wa2, ss2, zm2, 0, lv2.tiles, use_last)

    loads[5].wait()
    n2 = lv2.half
    for t in range(lv2.tiles):
        e2, o2, e3 = up2[t, 0, 0:n2], up2[t, 1, 0:n2], up2[t, 0, 1 : n2 + 1]
        zp1[t, pl.ds(0, n2, stride=2)] = e2
        zp1[t, pl.ds(1, n2, stride=2)] = o2
        zp1[t, pl.ds(lv1.half, n2, stride=2)] = 0.375 * e2 + 0.75 * o2 - 0.125 * e3
        zp1[t, pl.ds(lv1.half + 1, n2, stride=2)] = 0.75 * o2 + 0.375 * e3 - 0.125 * e2
        zh1[t], zl1[t] = split(zp1[t])
    for t in range(lv2.tiles):
        n_in = min(2, lv2.tiles - t)
        w = wp1[: n_in * LANES]
        e = jnp.dot(
            jnp.concatenate([zh1[t + i] for i in range(n_in)], axis=1), w,
            preferred_element_type=F32,
        ) + jnp.dot(
            jnp.concatenate([zl1[t + i] for i in range(n_in)], axis=1), w,
            preferred_element_type=F32,
        )
        for k in range(ratio):
            to = ratio * t + k
            if to < n1:
                for par in range(2):
                    rows = slice(par * lv1.half, par * lv1.half + lv1.half)
                    v = e[rows, LANES * k : LANES * k + LANES] * (
                        wide(mk1[to], lv1.half) * zm1[par]
                    )
                    d1[to + 1, rows] = v
                    acc1[to, rows] += v

    def use_up1(t, par, rows, av, edge):
        r = r1[t, rows] - av
        r1[t, rows] = r
        d1[t + 1, rows] = masked(wide(iv1[t, par], n_rows(rows)) * r, edge)

    def use_final1(t, par, rows, av, edge):
        r = r1[t, rows] - av
        c1[t + 2, rows] = (acc1[t, rows] + (1.0 + KEEP) * d1[t + 1, rows]) + masked(
            (RATIO * wide(iv1[t, par], n_rows(rows))) * r, edge
        )

    stage(lv1, d1, hh1, hl1, 0, n1)
    sweep(lv1, hh1, hl1, wa1, ss1, zm1, 0, n1, use_up1)
    stage(lv1, d1, hh1, hl1, 0, n1)
    sweep(lv1, hh1, hl1, wa1, ss1, zm1, 0, n1, use_final1)

    up = 2 * lv1.group // lv0.group
    tau_lo = (lo_b - own_lo) // up
    tau_hi = (lo_b + n_b - 1 - own_lo) // up
    n_tau = tau_hi + 2 - tau_lo
    jn = (lv0.half // 2 + 7) // 8 * 8
    lane_j = lax.broadcasted_iota(jnp.int32, (jn, LANES), 1) // gs
    bad = ((lane_j == 0) & (own_y == 0)) | ((lane_j == 2) & (own_y == wy - 1))
    turn = lax.rem(1 - own_y + wyp, wyp) * gs
    first = ZR // 2 - zh // 2
    loads[6].wait()
    for i in range(n_tau):
        at = own_x * per + (tau_lo + i + 2)

        def rows_of(par, start):
            v = pltpu.roll(c1[at, pl.ds(par * lv1.half + start, jn)], turn, 1)
            return jnp.where(bad, 0.0, v)

        e2, o2, e3 = rows_of(0, first), rows_of(1, first), rows_of(0, first + 1)
        zp0[i, pl.ds(0, jn, stride=2)] = e2
        zp0[i, pl.ds(1, jn, stride=2)] = o2
        zp0[i, pl.ds(lv0.half, jn, stride=2)] = 0.375 * e2 + 0.75 * o2 - 0.125 * e3
        zp0[i, pl.ds(lv0.half + 1, jn, stride=2)] = 0.75 * o2 + 0.375 * e3 - 0.125 * e2
        zh0[i], zl0[i] = split(zp0[i, 0 : lv0.rows])
    for i in range(n_tau - 1):
        e = jnp.dot(
            jnp.concatenate([zh0[i], zh0[i + 1]], axis=1), wp0[...],
            preferred_element_type=F32,
        ) + jnp.dot(
            jnp.concatenate([zl0[i], zl0[i + 1]], axis=1), wp0[...],
            preferred_element_type=F32,
        )
        for k in range(up):
            t = own_lo + up * (tau_lo + i) + k
            if lo_b <= t < lo_b + n_b:
                for par in range(2):
                    rows = slice(par * lv0.half, par * lv0.half + lv0.half)
                    v = e[rows, LANES * k : LANES * k + LANES] * (
                        wide(mk0[t], lv0.half) * zm0[par]
                    )
                    d0[t + 1, rows] = v
                    if own(t):
                        acc0[t - own_lo, rows] += v

    def use_up(t, par, rows, av, edge):
        r = r0[t, rows] - av
        r0[t, rows] = r
        d0[t + 1, rows] = masked(wide(iv0[t, par], n_rows(rows)) * r, edge)

    def use_final(t, par, rows, av, edge):
        r = r0[t, rows] - av
        acc0[t - own_lo, rows] += (1.0 + KEEP) * d0[t + 1, rows] + (
            RATIO * wide(iv0[t, par], n_rows(rows))
        ) * r

    lo_c, n_c = reach(2, 1)
    stage(lv0, d0, hh0, hl0, lo_c, n_c)
    sweep(lv0, hh0, hl0, wa0, ss0, zm0, lo_c, n_c, use_up)
    stage(lv0, d0, hh0, hl0, own_lo, own_n)
    sweep(lv0, hh0, hl0, wa0, ss0, zm0, own_lo, own_n, use_final)

    for i in range(own_n):
        for par in range(2):
            lo = par * lv0.half + zh
            tmp[pl.ds(par, hb, stride=2)] = acc0[i, lo : lo + hb]
        v = tmp[...].T.reshape(lv0.group, yh0, bz)
        out_ref[lv0.group * i : lv0.group * i + lv0.group] = v[:, H : H + by]

    for n, off in enumerate(offs_xy):
        sent_if(off, halo_copies(n))
    for n, off in enumerate(offs_z):
        sent_if(off, z_copies(n))
    for n, off in enumerate(offs_g):
        sent_if(off, g_copies(n))
    for n, off in enumerate(offs_p):
        sent_if(off, p_copies(n))


def local(mesh_shape, u, b):
    nx, ny, nz = (mesh_shape[a] for a in ("gx", "gy", "gz"))
    bx, by, bz = u.shape
    cx, cy, cz = bx // 2, by // 2, bz // 2
    wx = nx if nx <= 2 * REACH + 1 else 2 * REACH + 1
    wy = ny if ny <= 2 * REACH + 1 else 2 * REACH + 1
    wyp = 4 if wy <= 4 else 8
    gs = LANES // wyp
    yh0 = by + 2 * H
    xg0 = LANES // yh0
    lv0 = Level(
        xg0, (bx + 2 * H) // xg0, yh0, (bz + 2 * H) // 2, lambda x, y: x * yh0 + y, H // 2
    )
    xg1 = gs // cy
    lv1 = Level(
        xg1, cx * wx // xg1, cy * wy, (cz + 2 * ZR) // 2,
        lambda x, y: (y // cy) * gs + x * cy + y % cy, ZR // 2,
    )
    y2 = cy * wy // 2
    yh2 = 16 if y2 <= 16 else 32
    xg2 = LANES // yh2
    lv2 = Level(
        xg2, -(-(cx * wx // 2) // xg2), y2, (cz + 2 * ZR) // 4, lambda x, y: x * yh2 + y,
        ZR // 4,
    )

    offs_xy = [(a, c, 0) for a in (-1, 0, 1) for c in (-1, 0, 1) if (a or c)]
    offs_xy = [o for o in offs_xy if (nx > 1 or not o[0]) and (ny > 1 or not o[1])]
    zs = (-1, 1) if nz > 1 else ()
    offs_z = [(0, 0, c) for c in zs]
    sx = wx - 1 if wx == nx else REACH
    sy = wy - 1 if wy == ny else REACH
    offs_g = [(a, 0, 0) for a in range(-sx, sx + 1) if a]
    offs_p = [(0, a, c) for a in range(-sy, sy + 1) for c in (0,) + zs if a or c]
    offs = (offs_xy, offs_z, offs_g, offs_p)

    own_lo = H // xg0
    lo_b = (H - 4) // xg0
    n_b = (H + bx - 1 + 3) // xg0 - lo_b + 1
    px = []
    for x in range(cx):
        for s, w in restrict_taps(x):
            f = H + 2 * x + s
            px.append(((0, x), f // xg0 - lo_b, f % xg0, w))
    py = [(y, H + 2 * y + s, w) for y in range(cy) for s, w in restrict_taps(y)]
    once = plane_matrix(n_b, 1, px, py, lv0.at, lambda x, y: x * cy + y)
    m_r0 = once + np.roll(once, LANES // 2, axis=1)

    r_lo, r_hi = (-3) // xg1, (2 * xg2 + 1) // xg1
    px = []
    for x in range(xg2):
        for s, w in restrict_taps(x):
            f = 2 * x + s
            px.append(((0, x), f // xg1 - r_lo, f % xg1, w))
    py = [
        (y, 2 * y + s, w) for y in range(y2) for s, w in restrict_taps(y)
        if 0 <= 2 * y + s < cy * wy
    ]
    m_r1 = plane_matrix(r_hi - r_lo + 1, 1, px, py, lv1.at, lv2.at)

    ratio = 2 * xg2 // xg1
    px = []
    for f in range(2 * xg2):
        for c, w in prolong_taps(f):
            px.append(((f // xg1, f % xg1), c // xg2, c % xg2, w))
    py = [
        (f, c, w) for f in range(cy * wy) for c, w in prolong_taps(f) if 0 <= c < y2
    ]
    m_p1 = plane_matrix(2, ratio, px, py, lv2.at, lv1.at)

    up = 2 * xg1 // xg0
    px = []
    for f in range(2 * xg1):
        for c, w in prolong_taps(f):
            px.append(((f // xg0, f % xg0), c // xg1, c % xg1, w))
    py = [
        (f + H, c + cy, w) for f in range(-H, by + H) for c, w in prolong_taps(f)
        if -cy <= c < 2 * cy
    ]
    m_p0 = plane_matrix(2, up, px, py, lv1.at, lv0.at)

    consts = tuple(
        to_bf16(m)
        for m in (
            operator_matrix(lv0), operator_matrix(lv1), operator_matrix(lv2),
            m_r0, m_r1, m_p1, m_p0,
        )
    )
    vm = lambda *s: pltpu.VMEM(s, F32)
    bm = lambda *s: pltpu.VMEM(s, BF16)
    dma = lambda *s: pltpu.SemaphoreType.DMA(s)

    def per_level(lv):
        t, n = lv.tiles, lv.rows
        return (
            vm(t + 2, n, LANES), vm(t, n, LANES), vm(t, n, LANES),
            bm(t + 2, n, LANES), bm(t + 2, n, LANES), vm(4, 4, lv.half + 16, LANES),
            vm(t, 2, 8, LANES), vm(t, 8, LANES), vm(2, lv.half, LANES),
        )

    p0, p1, p2 = per_level(lv0), per_level(lv1), per_level(lv2)
    tau_lo = (lo_b - own_lo) // up
    n_tau = (lo_b + n_b - 1 - own_lo) // up + 2 - tau_lo
    jn = (lv0.half // 2 + 7) // 8 * 8
    geo = (nx, ny, nz, bx, by, bz, wx, wy, wyp)
    return pl.pallas_call(
        functools.partial(kernel, geo, lv0, lv1, lv2, offs),
        out_shape=jax.ShapeDtypeStruct(u.shape, F32),
        in_specs=[pl.BlockSpec(memory_space=pltpu.VMEM)] * 2
        + [pl.BlockSpec(memory_space=pl.ANY)] * len(consts),
        out_specs=pl.BlockSpec(memory_space=pltpu.VMEM),
        scratch_shapes=[bm(*c.shape) for c in consts]
        + [
            vm(bx + 2 * H, yh0, bz), vm(bx + 2 * H, yh0, bz), vm(bz, LANES),
            vm(2, 2, lv0.tiles, H, LANES), vm(2, 2, lv0.tiles, H, LANES),
            *p0, *p1, vm(lv1.tiles + 4, lv1.rows, LANES), p2[0], p2[1], *p2[3:],
            vm(2, lv0.half, LANES), vm(2, lv1.half + 16, LANES), vm(cz // 2, LANES),
            vm(wx, cz // 2, LANES), vm(wy, wx, lv1.half, LANES),
            vm(lv2.tiles, 2, lv2.half + 8, LANES), vm(lv2.tiles, lv1.rows, LANES),
            vm(n_tau, lv0.half + 2 * jn, LANES),
            bm(lv2.tiles, lv1.rows, LANES), bm(lv2.tiles, lv1.rows, LANES),
            bm(n_tau, lv0.rows, LANES), bm(n_tau, lv0.rows, LANES),
            dma(len(consts)), dma(max(1, len(offs_xy)), 2), dma(max(1, len(offs_xy)), 2),
            dma(2), dma(2), dma(max(1, len(offs_g))), dma(max(1, len(offs_g))),
            dma(max(1, len(offs_p))), dma(max(1, len(offs_p))),
        ],
        compiler_params=pltpu.CompilerParams(
            collective_id=0, has_side_effects=True, vmem_limit_bytes=60 * 1024 * 1024
        ),
    )(u, b, *consts)


def solution(mesh):
    placed = P("gx", "gy", "gz")
    return jax.shard_map(
        functools.partial(local, dict(mesh.shape)), mesh=mesh,
        in_specs=(placed, placed), out_specs=placed, check_vma=False,
    )
```

time: 58.6 us -> 33.5 us (0.57); the launches traced: 57.7 us -> 33.3 us
  Pallas kernels: 56.1 us -> 31.7 us
    pallas_call x1, Pallas kernels: 56.1 us -> 31.7 us  [local(): pl.pallas_call(functools.partial(kernel, geo, lv0, lv1, lv2, offs), out_s...]
where the time goes in v1:
time: 33.5 us; the launch traced here: 33.3 us
  Pallas kernels  31.7 us (95%)
  local copies, waits for them, and re-layouts  1.57 us (5%)
    pallas_call x1, Pallas kernels, local(): pl.pallas_call(functools.partial(kernel, geo, lv0, lv1, lv2, offs), out_s...  31.7 us
    unnamed x1, local copies, waits for them, and re-layouts  1.57 us

profile of v1, /device:TPU:0, one launch (start us, length us, event | category | flops | bytes accessed | tf_op | source)
XLA Modules:
  0.0 33.3 jit_solution(15325529569190559278)
XLA Ops:
  0.0 31.7 %shard_map.91 = f32[16,16,128]{2,1,0:T(8,128)} custom-call(f32[16,16,128]{2,1,0:T(8,128)} %u_ref.1, f32[16,16,128]{2,1,0:T(8,128)} %b_ref.1, bf16[256,256]{1,0:T(8,128)(2,1)} %constant.14.clone.refs_0_, bf16[256,256]{1,0:T(8,128)(2,1)} %constant.15.clone.refs_1_, bf16[256,256]{1,0:T(8,128)(2,1)} %constant.16.clone.refs_2_, ...), custom_call_target="tpu_custom_call" | custom-call | tf_op jit(solution)/shard_map/pallas_call | solution.py:849
  31.8 1.6 %copy.11 = f32[16,16,128]{2,1,0:T(8,128)} copy(f32[16,16,128]{2,1,0:T(8,128)} %shard_map.91) | data formatting | bytes 262144

commit v2 on v1

--- a/solution.py
+++ b/solution.py
@@ -116,11 +116,9 @@
 
 
 def kernel(
-    geo, lv0, lv1, lv2, offs, u_ref, b_ref, *refs,
+    geo, lv0, lv1, lv2, parts, u_hbm, b_hbm, w_hbm, out_ref, *refs,
 ):
-    (wa0_h, wa1_h, wa2_h, wr0_h, wr1_h, wp1_h, wp0_h, out_ref,
-     wa0, wa1, wa2, wr0, wr1, wp1, wp0,
-     ue, be, tmp, strip_out, strip_in,
+    (wall, u_ref, b_ref, ue, be, tmp, pad, strip_out, strip_in,
      d0, r0, acc0, hh0, hl0, ss0, iv0, mk0, zm0,
      d1, r1, acc1, hh1, hl1, ss1, iv1, mk1, zm1, c1,
      d2, r2, hh2, hl2, ss2, iv2, mk2, zm2,
@@ -135,65 +133,115 @@
     start_y = 0 if full_y else iy - REACH
     own_x = ix if full_x else REACH
     own_y = iy if full_y else REACH
-    offs_xy, offs_z, offs_g, offs_p = offs
-
-    def there(off, sign=1):
+
+    def both(*oks):
         ok = None
-        for p, n, o in zip(place, counts, off):
-            if o:
-                q = p + sign * o
-                c = (q >= 0) & (q < n)
-                ok = c if ok is None else ok & c
+        for o in oks:
+            if o is not None:
+                ok = o if ok is None else ok & o
         return ok
 
-    def device(off):
-        return tuple(p + o for p, o in zip(place, off))
+    def when(ok, act):
+        if ok is None:
+            act()
+        else:
+            pl.when(ok)(act)
+
+    def unless(ok, act):
+        if ok is not None:
+            pl.when(jnp.logical_not(ok))(act)
+
+    def inside(axis, p):
+        return (p >= 0) & (p < counts[axis])
+
+    def shifted(axis, off):
+        if off == 0:
+            return (place[axis], None, place[axis], None)
+        to, source = place[axis] + off, place[axis] - off
+        return (to, inside(axis, to), source, inside(axis, source))
+
+    def line_steps(axis, full):
+        p, n = place[axis], counts[axis]
+        if full:
+            steps = []
+            for k in sorted(range(1, n), key=lambda k: min(k, n - k)):
+                to, source = lax.rem(p + k, n), lax.rem(p + n - k, n)
+                steps.append((to, None, source, None, p, source))
+            return steps
+        offs = sorted((o for o in range(-REACH, REACH + 1) if o), key=abs)
+        return [shifted(axis, o) + (REACH - o, REACH - o) for o in offs]
+
+    zq, half_c = ZR // 2, cz // 2
+    x_steps = line_steps(0, full_x)
+    y_steps = line_steps(1, full_y)
+    if nz == 2:
+        z_steps = [
+            (1 - iz, None, 1 - iz, None, 1 - iz,
+             pl.multiple_of((1 - iz) * (half_c - zq), 8),
+             pl.multiple_of(iz * (zq + half_c), 8))
+        ]
+    elif nz > 2:
+        z_steps = [
+            shifted(2, 1) + (1, half_c - zq, 0), shifted(2, -1) + (0, 0, zq + half_c)
+        ]
+    else:
+        z_steps = []
+    plane_steps = [
+        ((ix, ys[0], iz), ys[1], ys[3], ys[4], None) for ys in y_steps
+    ] + [
+        ((ix, iy, zs[0]), zs[1], zs[3], own_y, zs) for zs in z_steps
+    ] + [
+        ((ix, ys[0], zs[0]), both(ys[1], zs[1]), both(ys[3], zs[3]), ys[4], zs)
+        for zs in z_steps for ys in y_steps
+    ]
+    near = [0] + ([-1, 1] if nx > 1 else [])
+    side = [0] + ([-1, 1] if ny > 1 else [])
+    xy_offs = [(a, c) for a in near for c in side if a or c]
+
+    def xy_step(off):
+        xs, ys = shifted(0, off[0]), shifted(1, off[1])
+        return (xs[0], ys[0]), both(xs[1], ys[1]), both(xs[3], ys[3])
+
+    greet = [((st[0], iy, iz), st[1], st[3]) for st in x_steps]
+    greet += [(st[0], st[1], st[2]) for st in plane_steps]
+    for off in xy_offs:
+        if off[0]:
+            to, ok, ok_from = xy_step(off)
+            if off[1]:
+                greet.append((to + (iz,), ok, ok_from))
+            for zs in z_steps:
+                greet.append((to + (zs[0],), both(ok, zs[1]), both(ok_from, zs[3])))
 
     barrier = pltpu.get_barrier_semaphore()
     total = 0
-    for off in sorted(set(offs_xy + offs_z + offs_g + offs_p)):
-        ok = there(off)
-        total = total + ok.astype(jnp.int32)
-
-        @pl.when(ok)
-        def _():
-            pl.semaphore_signal(
-                barrier, inc=1, device_id=device(off), device_id_type=MESH
-            )
-
-    loads = [
-        pltpu.make_async_copy(s, d, wsem.at[n])
-        for n, (s, d) in enumerate(
-            ((wa0_h, wa0), (wr0_h, wr0), (wa1_h, wa1), (wr1_h, wr1), (wa2_h, wa2),
-             (wp1_h, wp1), (wp0_h, wp0))
-        )
-    ]
-    for c in loads:
-        c.start()
-
-    def remote(src, dst, ss, rs, off):
+    for to, ok, ok_from in greet:
+        total = total + (1 if ok_from is None else ok_from.astype(jnp.int32))
+
+        def signal():
+            pl.semaphore_signal(barrier, inc=1, device_id=to, device_id_type=MESH)
+
+        when(ok, signal)
+
+    load_u = pltpu.make_async_copy(u_hbm, u_ref, wsem.at[0])
+    load_b = pltpu.make_async_copy(b_hbm, b_ref, wsem.at[1])
+    load_w = pltpu.make_async_copy(w_hbm, wall, wsem.at[2])
+    load_u.start()
+    load_b.start()
+    load_w.start()
+
+    def remote(src, dst, ss, rs, to):
         return pltpu.make_async_remote_copy(
             src_ref=src, dst_ref=dst, send_sem=ss, recv_sem=rs,
-            device_id=device(off), device_id_type=MESH,
-        )
-
-    def start_if(off, copies):
-        @pl.when(there(off))
-        def _():
-            for c in copies:
-                c.start()
-
-    def recv_if(off, copies):
-        @pl.when(there(off, -1))
-        def _():
-            for c in copies:
-                c.wait_recv()
-
-    def sent_if(off, copies):
-        @pl.when(there(off))
-        def _():
-            for c in copies:
-                c.wait_send()
+            device_id=to, device_id_type=MESH,
+        )
+
+    def weights(name):
+        blocks = []
+        for row, lane, rows, lanes in parts[name]:
+            blocks.append(wall[row : row + rows, lane : lane + lanes])
+        if parts[name][0][3] == LANES:
+            return jnp.concatenate(blocks, axis=0)
+        return jnp.concatenate(blocks, axis=1)
 
     def cut(off, size, low, high):
         if off == 0:
@@ -213,23 +261,72 @@
     def zero(ref, *at):
         ref[at] = jnp.zeros_like(ref[at])
 
-    def halo_copies(n, which=(0, 1)):
-        off = offs_xy[n]
-        res = []
-        for k in which:
-            ref, ext, sx, tx, sy, ty = halo_cut(off, k)
-            res.append(
-                remote(
-                    ref.at[sx, sy], ext.at[tx, ty], xysend.at[n, k], xyrecv.at[n, k], off
+    def halo_copy(n, k):
+        ref, ext, sx, tx, sy, ty = halo_cut(xy_offs[n], k)
+        to = xy_step(xy_offs[n])[0] + (iz,)
+        return remote(ref.at[sx, sy], ext.at[tx, ty], xysend.at[n, k], xyrecv.at[n, k], to)
+
+    yh0 = by + 2 * H
+    zh, hb = H // 2, bz // 2
+    own_lo, own_n = H // lv0.group, bx // lv0.group
+    edge_n = H // lv0.group
+    spots = [(a, c) for a in near for c in side]
+
+    def variant(c):
+        return 0 if c == 0 else (1 if c > 0 else 2)
+
+    def strip_cut(a):
+        if a == 0:
+            return slice(0, own_n), slice(own_lo, own_lo + own_n)
+        if a > 0:
+            return slice(own_n - edge_n, own_n), slice(0, edge_n)
+        return slice(0, edge_n), slice(own_lo + own_n, own_lo + own_n + edge_n)
+
+    def strip_copy(n, m):
+        a, c = spots[n]
+        zs = z_steps[m]
+        src, dst = strip_cut(a)
+        v, k = variant(c), zs[4]
+        to = (shifted(0, a)[0], shifted(1, c)[0], zs[0])
+        return remote(
+            strip_out.at[k, v, :, src], strip_in.at[k, v, :, dst],
+            zsend.at[n, m], zrecv.at[n, m], to,
+        )
+
+    def strip_ok(n, m, at):
+        a, c = spots[n]
+        return both(shifted(0, a)[at], shifted(1, c)[at], z_steps[m][at])
+
+    zero(pad, slice(None), slice(0, H))
+    zero(pad, slice(None), slice(H + by, yh0))
+    lane_y = lax.broadcasted_iota(jnp.int32, (2 * zh, LANES), 1) % yh0
+    load_u.wait()
+    load_b.wait()
+    for k, ref in enumerate((u_ref, b_ref)):
+        for t in range(own_n):
+            pad[:, H : H + by] = ref[lv0.group * t : lv0.group * t + lv0.group]
+            tmp[...] = pad[...].reshape(LANES, bz).T
+            for s, start in ((0, 0), (1, bz - H)):
+                v = jnp.concatenate(
+                    [tmp[pl.ds(start + par, zh, stride=2)] for par in range(2)], axis=0
                 )
-            )
-        return res
+                strip_out[s, 0, k, t] = v
+                if ny > 1:
+                    strip_out[s, 1, k, t] = jnp.where(
+                        lane_y < H, pltpu.roll(v, LANES - by, 1), 0.0
+                    )
+                    strip_out[s, 2, k, t] = jnp.where(
+                        lane_y >= H + by, pltpu.roll(v, by, 1), 0.0
+                    )
 
     pl.semaphore_wait(barrier, total)
-    for n, off in enumerate(offs_xy):
-        start_if(off, halo_copies(n, (0,)))
-    for n, off in enumerate(offs_xy):
-        start_if(off, halo_copies(n, (1,)))
+    for n, off in enumerate(xy_offs):
+        when(xy_step(off)[1], lambda: halo_copy(n, 0).start())
+    for m in range(len(z_steps)):
+        for n in range(len(spots)):
+            when(strip_ok(n, m, 1), lambda: strip_copy(n, m).start())
+    for n, off in enumerate(xy_offs):
+        when(xy_step(off)[1], lambda: halo_copy(n, 1).start())
 
     ue[H : H + bx, H : H + by] = u_ref[...]
     be[H : H + bx, H : H + by] = b_ref[...]
@@ -237,43 +334,41 @@
         for at in (slice(0, H - low), slice(H + bx + high, 2 * H + bx)):
             if at.stop > at.start:
                 zero(ext, at)
-    for off in [(a, c, 0) for a in (-1, 0, 1) for c in (-1, 0, 1) if a or c]:
+    for off in [(a, c) for a in (-1, 0, 1) for c in (-1, 0, 1) if a or c]:
 
         def clear():
             for k in range(2):
                 _, ext, _, tx, _, ty = halo_cut(off, k)
                 zero(ext, tx, ty)
 
-        if off in offs_xy:
-            pl.when(jnp.logical_not(there(off, -1)))(clear)
+        if off in xy_offs:
+            unless(xy_step(off)[2], clear)
         else:
             clear()
-    zq, half_c = ZR // 2, cz // 2
-    for side, rows in ((-1, slice(zq + half_c, 2 * zq + half_c)), (1, slice(0, zq))):
+    for s, rows in ((0, slice(zq + half_c, 2 * zq + half_c)), (1, slice(0, zq))):
+        z_ok = inside(2, iz + (1 - 2 * s)) if nz > 1 else None
+        for a in (-1, 0, 1):
+            for c in (-1, 0, 1):
+
+                def clear():
+                    zero(strip_in, s, variant(c), slice(None), strip_cut(a)[1])
+
+                if (a, c) in spots and nz > 1:
+                    unless(both(shifted(0, a)[3], shifted(1, c)[3], z_ok), clear)
+                else:
+                    clear()
 
         def clear():
-            zero(strip_in, (side + 1) // 2)
             zero(land, slice(None), slice(None), rows)
 
         if nz > 1:
-            pl.when(jnp.logical_not(there((0, 0, side), -1)))(clear)
+            unless(z_ok, clear)
         else:
             clear()
-    if not full_x:
-        for off in offs_g:
-
-            @pl.when(jnp.logical_not(there(off, -1)))
-            def _():
-                zero(line, REACH - off[0])
-
-    if not full_y:
-        for off in offs_p:
-            if off[2] == 0:
-
-                @pl.when(jnp.logical_not(there(off, -1)))
-                def _():
-                    zero(land, REACH - off[1])
-
+    for st in x_steps:
+        unless(st[3], lambda: zero(land, slice(None), st[5]))
+    for st in y_steps:
+        unless(st[3], lambda: zero(land, st[5]))
 
     def set_up(lv, level, iv, mk, zm, d, ss, x_first, y_first, z_first, x_at, y_at):
         lane = lax.broadcasted_iota(jnp.int32, (8, LANES), 1)
@@ -307,7 +402,6 @@
         ss[:, :, 8 + lv.half :] = jnp.zeros_like(ss[:, :, 8 + lv.half :])
 
     gs = LANES // wyp
-    yh0 = by + 2 * H
     set_up(
         lv0, 0, iv0, mk0, zm0, d0, ss0, ix * bx - H, iy * by - H, iz * bz - H,
         lambda n: n // yh0, lambda n: n % yh0,
@@ -327,45 +421,39 @@
     xs1[:, 8 + lv1.half :] = jnp.zeros_like(xs1[:, 8 + lv1.half :])
     up2[...] = jnp.zeros_like(up2)
 
-    zh = H // 2
-    hb = bz // 2
-
-    def turned(ext, t):
-        tmp[...] = ext[lv0.group * t : lv0.group * t + lv0.group].reshape(LANES, bz).T
-        return tmp[pl.ds(0, hb, stride=2)], tmp[pl.ds(1, hb, stride=2)]
-
-    def strips(n, t, par, val):
-        lo, hi = par * zh, par * zh + zh
-        strip_out[0, n, t, lo:hi] = val[:zh]
-        strip_out[1, n, t, lo:hi] = val[hb - zh :]
-
-    def z_copies(n):
-        off = offs_z[n]
-        k = 1 if off[2] > 0 else 0
-        return [remote(strip_out.at[k], strip_in.at[k], zsend.at[k], zrecv.at[k], off)]
-
-    for k, ext in enumerate((ue, be)):
-        for n, off in enumerate(offs_xy):
-            recv_if(off, halo_copies(n, (k,)))
+    def turn_field(k):
+        ext = (ue, be)[k]
+        for n, off in enumerate(xy_offs):
+            when(xy_step(off)[2], lambda: halo_copy(n, k).wait_recv())
         for t in range(lv0.tiles):
-            for par, val in enumerate(turned(ext, t)):
+            tmp[...] = ext[lv0.group * t : lv0.group * t + lv0.group].reshape(LANES, bz).T
+            for par in range(2):
+                val = tmp[pl.ds(par, hb, stride=2)]
                 lo = par * lv0.half + zh
-                strips(k, t, par, val)
                 if k == 0:
                     d0[t + 1, lo : lo + hb] = val
                 else:
                     r0[t, lo : lo + hb] = UNIT * val
-    for n, off in enumerate(offs_z):
-        start_if(off, z_copies(n))
-    for n, off in enumerate(offs_z):
-        recv_if(off, z_copies(n))
-    for t in range(lv0.tiles):
-        for par in range(2):
-            for side in range(2):
-                lo = par * lv0.half + (0 if side else zh + hb)
-                rows = slice(lo, lo + zh)
-                d0[t + 1, rows] = strip_in[side, 0, t, par * zh : par * zh + zh]
-                r0[t, rows] = UNIT * strip_in[side, 1, t, par * zh : par * zh + zh]
+
+    def fill_strips():
+        for t in range(lv0.tiles):
+            for s in range(2):
+                for k in range(2):
+                    v = (strip_in[s, 0, k, t] + strip_in[s, 1, k, t]) + strip_in[s, 2, k, t]
+                    for par in range(2):
+                        lo = par * lv0.half + (0 if s else zh + hb)
+                        rows, part = slice(lo, lo + zh), v[par * zh : par * zh + zh]
+                        if k == 0:
+                            d0[t + 1, rows] = part
+                        else:
+                            r0[t, rows] = UNIT * part
+
+    turn_field(0)
+    for m in range(len(z_steps)):
+        for n in range(len(spots)):
+            when(strip_ok(n, m, 3), lambda: strip_copy(n, m).wait_recv())
+    fill_strips()
+    turn_field(1)
 
     def stage(lv, d, hh, hl, lo, count):
         step = 48 if lv.rows % 48 == 0 else min(lv.rows, 64)
@@ -402,8 +490,8 @@
                     axis=1,
                 )
 
-            s = jnp.dot(lhs(hh), w[...], preferred_element_type=F32) + jnp.dot(
-                lhs(hl), w[...], preferred_element_type=F32
+            s = jnp.dot(lhs(hh), w, preferred_element_type=F32) + jnp.dot(
+                lhs(hl), w, preferred_element_type=F32
             )
             for k in range(size):
                 slot = (i % 2) * 2 + k if isinstance(i, int) else k
@@ -442,9 +530,6 @@
     def n_rows(rows):
         return rows.stop - rows.start
 
-    own_lo = H // lv0.group
-    own_n = bx // lv0.group
-
     def own(t):
         return own_lo <= t < own_lo + own_n
 
@@ -476,13 +561,13 @@
 
     lo_a, n_a = reach(6, 5)
     lo_b, n_b = reach(4, 3)
-    loads[0].wait()
+    load_w.wait()
     stage(lv0, d0, hh0, hl0, lo_a, n_a)
-    sweep(lv0, hh0, hl0, wa0, ss0, zm0, lo_a, n_a, use_residual)
+    sweep(lv0, hh0, hl0, weights('wa0'), ss0, zm0, lo_a, n_a, use_residual)
     stage(lv0, d0, hh0, hl0, lo_b, n_b)
-    sweep(lv0, hh0, hl0, wa0, ss0, zm0, lo_b, n_b, use_step)
+    sweep(lv0, hh0, hl0, weights('wa0'), ss0, zm0, lo_b, n_b, use_step)
     stage(lv0, d0, hh0, hl0, lo_b, n_b)
-    sweep(lv0, hh0, hl0, wa0, ss0, zm0, lo_b, n_b, use_down)
+    sweep(lv0, hh0, hl0, weights('wa0'), ss0, zm0, lo_b, n_b, use_down)
 
     def restricted(parts, w):
         hi, lo = zip(*[split(p) for p in parts])
@@ -490,8 +575,7 @@
             jnp.concatenate(hi, axis=1), w, preferred_element_type=F32
         ) + jnp.dot(jnp.concatenate(lo, axis=1), w, preferred_element_type=F32)
 
-    loads[1].wait()
-    x = restricted([r0[lo_b + i] for i in range(n_b)], wr0[...])
+    x = restricted([r0[lo_b + i] for i in range(n_b)], weights('wr0'))
     xs0[0] = x[: lv0.half]
     xs0[1] = x[lv0.half :]
     def pick(ref, par, start, n):
@@ -513,39 +597,41 @@
     packed = jnp.where(lane_c < LANES // 2, even, odd)
     blk[...] = packed
 
-    def slot(axis, off):
-        if (full_x, full_y)[axis]:
-            return (ix, iy)[axis]
-        return REACH - off
-
-    def g_copies(n):
-        off = offs_g[n]
-        return [remote(blk, line.at[slot(0, off[0])], gsend.at[n], grecv.at[n], off)]
-
-    def p_copies(n):
-        off = offs_p[n]
-        if off[2] == 0:
-            src, dst = slice(0, half_c), slice(zq, zq + half_c)
-        elif off[2] > 0:
-            src, dst = slice(half_c - zq, half_c), slice(0, zq)
+    def g_copy(n):
+        st = x_steps[n]
+        return remote(blk, line.at[st[4]], gsend.at[n], grecv.at[n], (st[0], iy, iz))
+
+    def p_copy(n, m, jx):
+        to, _, _, jy, zs = plane_steps[n]
+        if zs is None:
+            src, dst = pl.ds(0, half_c), pl.ds(zq, half_c)
         else:
-            src, dst = slice(0, zq), slice(zq + half_c, 2 * zq + half_c)
-        return [
-            remote(
-                line.at[:, src], land.at[slot(1, off[1]), :, dst], psend.at[n], precv.at[n], off
-            )
-        ]
-
-    for n, off in enumerate(offs_g):
-        start_if(off, g_copies(n))
-    line[own_x] = packed
-    for n, off in enumerate(offs_g):
-        recv_if(off, g_copies(n))
-    for n, off in enumerate(offs_p):
-        start_if(off, p_copies(n))
-    land[own_y, :, zq : zq + half_c] = line[...]
-    for n, off in enumerate(offs_p):
-        recv_if(off, p_copies(n))
+            src, dst = pl.ds(zs[5], zq), pl.ds(zs[6], zq)
+        from_ref = blk if m == 0 else line.at[jx]
+        return remote(
+            from_ref.at[src], land.at[jy, jx, dst], psend.at[n, m], precv.at[n, m], to
+        )
+
+    sources = [(None, own_x)] + [(st[3], st[5]) for st in x_steps]
+    for n, st in enumerate(x_steps):
+        when(st[1], lambda: g_copy(n).start())
+    for m, (ok, jx) in enumerate(sources):
+
+        def act():
+            if m:
+                g_copy(m - 1).wait_recv()
+            for n, st in enumerate(plane_steps):
+                when(st[1], lambda: p_copy(n, m, jx).start())
+            land[own_y, jx, zq : zq + half_c] = packed if m == 0 else line[jx]
+
+        when(ok, act)
+    for m, (ok, jx) in enumerate(sources):
+
+        def act():
+            for n, st in enumerate(plane_steps):
+                when(st[2], lambda: p_copy(n, m, jx).wait_recv())
+
+        when(ok, act)
 
     per = cx // lv1.group
     lane_h = lax.broadcasted_iota(jnp.int32, (lv1.half, LANES), 1) // gs
@@ -584,17 +670,16 @@
     def use_down1(t, par, rows, av, edge):
         r1[t, rows] = masked((r1[t, rows] - av) * wide(mk1[t], n_rows(rows)), edge)
 
-    loads[2].wait()
     n1 = lv1.tiles
     stage(lv1, d1, hh1, hl1, 0, n1)
-    sweep(lv1, hh1, hl1, wa1, ss1, zm1, 0, n1, use_step1)
+    sweep(lv1, hh1, hl1, weights('wa1'), ss1, zm1, 0, n1, use_step1)
     stage(lv1, d1, hh1, hl1, 0, n1)
-    sweep(lv1, hh1, hl1, wa1, ss1, zm1, 0, n1, use_down1)
+    sweep(lv1, hh1, hl1, weights('wa1'), ss1, zm1, 0, n1, use_down1)
 
     ratio = 2 * lv2.group // lv1.group
     r_lo = (-3) // lv1.group
     r_hi = (2 * lv2.group + 1) // lv1.group
-    loads[3].wait()
+    wr1 = weights('wr1')
     for t in range(lv2.tiles):
         a, e = max(0, ratio * t + r_lo), min(n1 - 1, ratio * t + r_hi)
         skip = (a - (ratio * t + r_lo)) * LANES
@@ -614,12 +699,11 @@
         lo = rows.start - par * lv2.half
         up2[t, par, lo : lo + n_rows(rows)] = (1.0 + KEEP) * d2[t + 1, rows] + step
 
-    loads[4].wait()
     stage(lv2, d2, hh2, hl2, 0, lv2.tiles)
-    sweep(lv2, hh2, hl2, wa2, ss2, zm2, 0, lv2.tiles, use_last)
-
-    loads[5].wait()
+    sweep(lv2, hh2, hl2, weights('wa2'), ss2, zm2, 0, lv2.tiles, use_last)
+
     n2 = lv2.half
+    wp1 = weights('wp1')
     for t in range(lv2.tiles):
         e2, o2, e3 = up2[t, 0, 0:n2], up2[t, 1, 0:n2], up2[t, 0, 1 : n2 + 1]
         zp1[t, pl.ds(0, n2, stride=2)] = e2
@@ -660,9 +744,9 @@
         )
 
     stage(lv1, d1, hh1, hl1, 0, n1)
-    sweep(lv1, hh1, hl1, wa1, ss1, zm1, 0, n1, use_up1)
+    sweep(lv1, hh1, hl1, weights('wa1'), ss1, zm1, 0, n1, use_up1)
     stage(lv1, d1, hh1, hl1, 0, n1)
-    sweep(lv1, hh1, hl1, wa1, ss1, zm1, 0, n1, use_final1)
+    sweep(lv1, hh1, hl1, weights('wa1'), ss1, zm1, 0, n1, use_final1)
 
     up = 2 * lv1.group // lv0.group
     tau_lo = (lo_b - own_lo) // up
@@ -673,7 +757,7 @@
     bad = ((lane_j == 0) & (own_y == 0)) | ((lane_j == 2) & (own_y == wy - 1))
     turn = lax.rem(1 - own_y + wyp, wyp) * gs
     first = ZR // 2 - zh // 2
-    loads[6].wait()
+    wp0 = weights('wp0')
     for i in range(n_tau):
         at = own_x * per + (tau_lo + i + 2)
 
@@ -689,10 +773,10 @@
         zh0[i], zl0[i] = split(zp0[i, 0 : lv0.rows])
     for i in range(n_tau - 1):
         e = jnp.dot(
-            jnp.concatenate([zh0[i], zh0[i + 1]], axis=1), wp0[...],
+            jnp.concatenate([zh0[i], zh0[i + 1]], axis=1), wp0,
             preferred_element_type=F32,
         ) + jnp.dot(
-            jnp.concatenate([zl0[i], zl0[i + 1]], axis=1), wp0[...],
+            jnp.concatenate([zl0[i], zl0[i + 1]], axis=1), wp0,
             preferred_element_type=F32,
         )
         for k in range(up):
@@ -720,9 +804,9 @@
 
     lo_c, n_c = reach(2, 1)
     stage(lv0, d0, hh0, hl0, lo_c, n_c)
-    sweep(lv0, hh0, hl0, wa0, ss0, zm0, lo_c, n_c, use_up)
+    sweep(lv0, hh0, hl0, weights('wa0'), ss0, zm0, lo_c, n_c, use_up)
     stage(lv0, d0, hh0, hl0, own_lo, own_n)
-    sweep(lv0, hh0, hl0, wa0, ss0, zm0, own_lo, own_n, use_final)
+    sweep(lv0, hh0, hl0, weights('wa0'), ss0, zm0, own_lo, own_n, use_final)
 
     for i in range(own_n):
         for par in range(2):
@@ -731,14 +815,21 @@
         v = tmp[...].T.reshape(lv0.group, yh0, bz)
         out_ref[lv0.group * i : lv0.group * i + lv0.group] = v[:, H : H + by]
 
-    for n, off in enumerate(offs_xy):
-        sent_if(off, halo_copies(n))
-    for n, off in enumerate(offs_z):
-        sent_if(off, z_copies(n))
-    for n, off in enumerate(offs_g):
-        sent_if(off, g_copies(n))
-    for n, off in enumerate(offs_p):
-        sent_if(off, p_copies(n))
+    for n, off in enumerate(xy_offs):
+        for k in range(2):
+            when(xy_step(off)[1], lambda: halo_copy(n, k).wait_send())
+    for m in range(len(z_steps)):
+        for n in range(len(spots)):
+            when(strip_ok(n, m, 1), lambda: strip_copy(n, m).wait_send())
+    for n, st in enumerate(x_steps):
+        when(st[1], lambda: g_copy(n).wait_send())
+    for m, (ok, jx) in enumerate(sources):
+
+        def act():
+            for n, st in enumerate(plane_steps):
+                when(st[1], lambda: p_copy(n, m, jx).wait_send())
+
+        when(ok, act)
 
 
 def local(mesh_shape, u, b):
@@ -767,16 +858,6 @@
         ZR // 4,
     )
 
-    offs_xy = [(a, c, 0) for a in (-1, 0, 1) for c in (-1, 0, 1) if (a or c)]
-    offs_xy = [o for o in offs_xy if (nx > 1 or not o[0]) and (ny > 1 or not o[1])]
-    zs = (-1, 1) if nz > 1 else ()
-    offs_z = [(0, 0, c) for c in zs]
-    sx = wx - 1 if wx == nx else REACH
-    sy = wy - 1 if wy == ny else REACH
-    offs_g = [(a, 0, 0) for a in range(-sx, sx + 1) if a]
-    offs_p = [(0, a, c) for a in range(-sy, sy + 1) for c in (0,) + zs if a or c]
-    offs = (offs_xy, offs_z, offs_g, offs_p)
-
     own_lo = H // xg0
     lo_b = (H - 4) // xg0
     n_b = (H + bx - 1 + 3) // xg0 - lo_b + 1
@@ -822,13 +903,27 @@
     ]
     m_p0 = plane_matrix(2, up, px, py, lv1.at, lv0.at)
 
-    consts = tuple(
-        to_bf16(m)
-        for m in (
-            operator_matrix(lv0), operator_matrix(lv1), operator_matrix(lv2),
-            m_r0, m_r1, m_p1, m_p0,
-        )
-    )
+    parts, stack, row = {}, [], 0
+    for name, m in (
+        ("wa0", operator_matrix(lv0)), ("wa1", operator_matrix(lv1)),
+        ("wa2", operator_matrix(lv2)), ("wr0", m_r0), ("wr1", m_r1), ("wp1", m_p1),
+        ("wp0", m_p0),
+    ):
+        if m.shape[1] == LANES:
+            m = np.pad(m, ((0, m.shape[0] % 2), (0, 0)))
+            half = m.shape[0] // 2
+            assert half % 16 == 0
+            parts[name] = [(row, 0, half, LANES), (row, LANES, half, LANES)]
+            stack.append(np.concatenate([m[:half], m[half:]], axis=1))
+            row += half
+        else:
+            parts[name] = []
+            for c in range(0, m.shape[1], 256):
+                parts[name].append((row, 0, m.shape[0], min(256, m.shape[1] - c)))
+                piece = m[:, c : c + 256]
+                stack.append(np.pad(piece, ((0, 0), (0, 256 - piece.shape[1]))))
+                row += m.shape[0]
+    consts = to_bf16(np.concatenate(stack, axis=0))
     vm = lambda *s: pltpu.VMEM(s, F32)
     bm = lambda *s: pltpu.VMEM(s, BF16)
     dma = lambda *s: pltpu.SemaphoreType.DMA(s)
@@ -846,16 +941,22 @@
     n_tau = (lo_b + n_b - 1 - own_lo) // up + 2 - tau_lo
     jn = (lv0.half // 2 + 7) // 8 * 8
     geo = (nx, ny, nz, bx, by, bz, wx, wy, wyp)
+    near, side = (3 if nx > 1 else 1), (3 if ny > 1 else 1)
+    n_z = 0 if nz == 1 else 1 if nz == 2 else 2
+    n_x = max(1, nx - 1 if wx == nx else 2 * REACH)
+    n_y = ny - 1 if wy == ny else 2 * REACH
+    n_p = max(1, (n_y + 1) * (n_z + 1) - 1)
+    n_xy, n_s = max(1, near * side - 1), near * side
     return pl.pallas_call(
-        functools.partial(kernel, geo, lv0, lv1, lv2, offs),
+        functools.partial(kernel, geo, lv0, lv1, lv2, parts),
         out_shape=jax.ShapeDtypeStruct(u.shape, F32),
-        in_specs=[pl.BlockSpec(memory_space=pltpu.VMEM)] * 2
-        + [pl.BlockSpec(memory_space=pl.ANY)] * len(consts),
+        in_specs=[pl.BlockSpec(memory_space=pl.ANY)] * 3,
         out_specs=pl.BlockSpec(memory_space=pltpu.VMEM),
-        scratch_shapes=[bm(*c.shape) for c in consts]
-        + [
+        scratch_shapes=[
+            bm(*consts.shape), vm(bx, by, bz), vm(bx, by, bz),
             vm(bx + 2 * H, yh0, bz), vm(bx + 2 * H, yh0, bz), vm(bz, LANES),
-            vm(2, 2, lv0.tiles, H, LANES), vm(2, 2, lv0.tiles, H, LANES),
+            vm(xg0, yh0, bz), vm(2, 3, 2, bx // xg0, H, LANES),
+            vm(2, 3, 2, lv0.tiles, H, LANES),
             *p0, *p1, vm(lv1.tiles + 4, lv1.rows, LANES), p2[0], p2[1], *p2[3:],
             vm(2, lv0.half, LANES), vm(2, lv1.half + 16, LANES), vm(cz // 2, LANES),
             vm(wx, cz // 2, LANES), vm(wy, wx, lv1.half, LANES),
@@ -863,14 +964,13 @@
             vm(n_tau, lv0.half + 2 * jn, LANES),
             bm(lv2.tiles, lv1.rows, LANES), bm(lv2.tiles, lv1.rows, LANES),
             bm(n_tau, lv0.rows, LANES), bm(n_tau, lv0.rows, LANES),
-            dma(len(consts)), dma(max(1, len(offs_xy)), 2), dma(max(1, len(offs_xy)), 2),
-            dma(2), dma(2), dma(max(1, len(offs_g))), dma(max(1, len(offs_g))),
-            dma(max(1, len(offs_p))), dma(max(1, len(offs_p))),
+            dma(3), dma(n_xy, 2), dma(n_xy, 2), dma(n_s, max(1, n_z)), dma(n_s, max(1, n_z)),
+            dma(n_x), dma(n_x), dma(n_p, n_x + 1), dma(n_p, n_x + 1),
         ],
         compiler_params=pltpu.CompilerParams(
             collective_id=0, has_side_effects=True, vmem_limit_bytes=60 * 1024 * 1024
         ),
-    )(u, b, *consts)
+    )(u, b, consts)
 
 
 def solution(mesh):

time: 33.5 us -> 30.5 us (0.910)
  Pallas kernels: 31.7 us -> 28.8 us
    pallas_call x1, Pallas kernels: 31.7 us -> 28.8 us  [local(): pl.pallas_call(functools.partial(kernel, geo, lv0, lv1, lv2, parts), out_...]
where the time goes in v2:
time: 30.5 us; the launch traced here: 30.3 us
  Pallas kernels  28.8 us (94%)
  local copies, waits for them, and re-layouts  1.57 us (5%)
    pallas_call x1, Pallas kernels, local(): pl.pallas_call(functools.partial(kernel, geo, lv0, lv1, lv2, parts), out_...  28.8 us
    unnamed x1, local copies, waits for them, and re-layouts  1.57 us

profile of v2, /device:TPU:0, one launch (start us, length us, event | category | flops | bytes accessed | tf_op | source)
XLA Modules:
  0.0 30.3 jit_solution(5629773506200619065)
XLA Ops:
  0.0 28.8 %shard_map.37 = f32[16,16,128]{2,1,0:T(8,128)} custom-call(f32[16,16,128]{2,1,0:T(8,128)} %u_hbm.1, f32[16,16,128]{2,1,0:T(8,128)} %b_hbm.1, bf16[2304,256]{1,0:T(8,128)(2,1)} %constant.2.clone.w_hbm), custom_call_target="tpu_custom_call" | custom-call | tf_op jit(solution)/shard_map/pallas_call | solution.py:950
  28.8 1.6 %copy.5 = f32[16,16,128]{2,1,0:T(8,128)} copy(f32[16,16,128]{2,1,0:T(8,128)} %shard_map.37) | data formatting | bytes 262144

commit v3 on v2

--- a/solution.py
+++ b/solution.py
@@ -320,13 +320,14 @@
                     )
 
     pl.semaphore_wait(barrier, total)
-    for n, off in enumerate(xy_offs):
-        when(xy_step(off)[1], lambda: halo_copy(n, 0).start())
     for m in range(len(z_steps)):
-        for n in range(len(spots)):
+        for n in sorted(range(len(spots)), key=lambda n: -abs(spots[n][0]) - abs(spots[n][1])):
             when(strip_ok(n, m, 1), lambda: strip_copy(n, m).start())
-    for n, off in enumerate(xy_offs):
-        when(xy_step(off)[1], lambda: halo_copy(n, 1).start())
+    far_first = sorted(range(len(xy_offs)), key=lambda n: -abs(xy_offs[n][0] * xy_offs[n][1]))
+    for n in far_first:
+        when(xy_step(xy_offs[n])[1], lambda: halo_copy(n, 0).start())
+    for n in far_first:
+        when(xy_step(xy_offs[n])[1], lambda: halo_copy(n, 1).start())
 
     ue[H : H + bx, H : H + by] = u_ref[...]
     be[H : H + bx, H : H + by] = b_ref[...]
@@ -433,27 +434,25 @@
                 if k == 0:
                     d0[t + 1, lo : lo + hb] = val
                 else:
-                    r0[t, lo : lo + hb] = UNIT * val
-
-    def fill_strips():
+                    r0[t, lo : lo + hb] = UNIT * val - r0[t, lo : lo + hb]
+
+    def fill_strips(k):
         for t in range(lv0.tiles):
             for s in range(2):
-                for k in range(2):
-                    v = (strip_in[s, 0, k, t] + strip_in[s, 1, k, t]) + strip_in[s, 2, k, t]
-                    for par in range(2):
-                        lo = par * lv0.half + (0 if s else zh + hb)
-                        rows, part = slice(lo, lo + zh), v[par * zh : par * zh + zh]
-                        if k == 0:
-                            d0[t + 1, rows] = part
-                        else:
-                            r0[t, rows] = UNIT * part
+                v = (strip_in[s, 0, k, t] + strip_in[s, 1, k, t]) + strip_in[s, 2, k, t]
+                for par in range(2):
+                    lo = par * lv0.half + (0 if s else zh + hb)
+                    rows, part = slice(lo, lo + zh), v[par * zh : par * zh + zh]
+                    if k == 0:
+                        d0[t + 1, rows] = part
+                    else:
+                        r0[t, rows] = UNIT * part - r0[t, rows]
 
     turn_field(0)
     for m in range(len(z_steps)):
         for n in range(len(spots)):
             when(strip_ok(n, m, 3), lambda: strip_copy(n, m).wait_recv())
-    fill_strips()
-    turn_field(1)
+    fill_strips(0)
 
     def stage(lv, d, hh, hl, lo, count):
         step = 48 if lv.rows % 48 == 0 else min(lv.rows, 64)
@@ -538,13 +537,18 @@
         hi = (H + bx - 1 + above) // lv0.group
         return lo, hi - lo + 1
 
-    def use_residual(t, par, rows, av, edge):
-        r = r0[t, rows] - av
-        r0[t, rows] = r
-        d = masked(wide(iv0[t, par], n_rows(rows)) * r, edge)
-        if own(t):
-            acc0[t - own_lo, rows] = d0[t + 1, rows] + d
-        d0[t + 1, rows] = d
+    def use_product(t, par, rows, av, edge):
+        r0[t, rows] = av
+
+    def first_step(t):
+        size = 24 if lv0.half % 24 == 0 else 8
+        for par in range(2):
+            for at in range(0, lv0.half, size):
+                rows = slice(par * lv0.half + at, par * lv0.half + at + size)
+                d = wide(iv0[t, par], size) * r0[t, rows] * zm0[par, at : at + size]
+                if own(t):
+                    acc0[t - own_lo, rows] = d0[t + 1, rows] + d
+                d0[t + 1, rows] = d
 
     def use_step(t, par, rows, av, edge):
         r = r0[t, rows] - av
@@ -563,7 +567,11 @@
     lo_b, n_b = reach(4, 3)
     load_w.wait()
     stage(lv0, d0, hh0, hl0, lo_a, n_a)
-    sweep(lv0, hh0, hl0, weights('wa0'), ss0, zm0, lo_a, n_a, use_residual)
+    sweep(lv0, hh0, hl0, weights('wa0'), ss0, zm0, lo_a, n_a, use_product)
+    turn_field(1)
+    fill_strips(1)
+    for t in range(lo_a, lo_a + n_a):
+        first_step(t)
     stage(lv0, d0, hh0, hl0, lo_b, n_b)
     sweep(lv0, hh0, hl0, weights('wa0'), ss0, zm0, lo_b, n_b, use_step)
     stage(lv0, d0, hh0, hl0, lo_b, n_b)
@@ -625,14 +633,6 @@
             land[own_y, jx, zq : zq + half_c] = packed if m == 0 else line[jx]
 
         when(ok, act)
-    for m, (ok, jx) in enumerate(sources):
-
-        def act():
-            for n, st in enumerate(plane_steps):
-                when(st[2], lambda: p_copy(n, m, jx).wait_recv())
-
-        when(ok, act)
-
     per = cx // lv1.group
     lane_h = lax.broadcasted_iota(jnp.int32, (lv1.half, LANES), 1) // gs
 
@@ -656,7 +656,14 @@
                 d1[t + 1, rows] = d
                 acc1[t, rows] = d
 
-    loop(wx, place_block, 4)
+    for m, (ok, jx) in enumerate(sources):
+
+        def act():
+            for n, st in enumerate(plane_steps):
+                when(st[2], lambda: p_copy(n, m, jx).wait_recv())
+
+        when(ok, act)
+        place_block(jx)
 
     def use_step1(t, par, rows, av, edge):
         r = r1[t, rows] - av
@@ -949,7 +956,7 @@
     n_xy, n_s = max(1, near * side - 1), near * side
     return pl.pallas_call(
         functools.partial(kernel, geo, lv0, lv1, lv2, parts),
-        out_shape=jax.ShapeDtypeStruct(u.shape, F32),
+        out_shape=pltpu.VMEM(u.shape, F32),
         in_specs=[pl.BlockSpec(memory_space=pl.ANY)] * 3,
         out_specs=pl.BlockSpec(memory_space=pltpu.VMEM),
         scratch_shapes=[

time: 30.5 us -> 27.8 us (0.911)
  Pallas kernels: 28.8 us -> 27 us
  local copies, waits for them, and re-layouts: 1.57 us -> 0.66 us
    pallas_call x1, Pallas kernels: 28.8 us -> 27 us  [local(): pl.pallas_call(functools.partial(kernel, geo, lv0, lv1, lv2, parts), out_...]
    unnamed x1, local copies, waits for them, and re-layouts: 1.57 us -> 0.66 us
where the time goes in v3:
time: 27.8 us; the launch traced here: 27.7 us
  Pallas kernels  27 us (97%)
  local copies, waits for them, and re-layouts  0.66 us (2%)
    pallas_call x1, Pallas kernels, local(): pl.pallas_call(functools.partial(kernel, geo, lv0, lv1, lv2, parts), out_...  27 us
    unnamed x1, local copies, waits for them, and re-layouts  0.66 us

profile of v3, /device:TPU:0, one launch (start us, length us, event | category | flops | bytes accessed | tf_op | source)
XLA Modules:
  0.0 27.7 jit_solution(5219443377750013013)
XLA Ops:
  0.0 27.0 %shard_map.37 = f32[16,16,128]{2,1,0:T(8,128)S(1)} custom-call(f32[16,16,128]{2,1,0:T(8,128)} %u_hbm.1, f32[16,16,128]{2,1,0:T(8,128)} %b_hbm.1, bf16[2304,256]{1,0:T(8,128)(2,1)} %constant.2.clone.w_hbm), custom_call_target="tpu_custom_call" | custom-call | tf_op jit(solution)/shard_map/pallas_call | solution.py:957
  27.0 0.7 %copy.5 = f32[16,16,128]{2,1,0:T(8,128)} copy(f32[16,16,128]{2,1,0:T(8,128)S(1)} %shard_map.37) | data formatting | bytes 262144

commit v4 on v3

--- a/solution.py
+++ b/solution.py
@@ -53,9 +53,9 @@
 
 
 class Level:
-    def __init__(self, group, tiles, height, half, at, parts):
+    def __init__(self, group, tiles, height, half, at, parts, pad):
         self.group, self.tiles, self.height, self.half, self.at = group, tiles, height, half, at
-        self.parts = parts
+        self.parts, self.pad = parts, pad
         self.rows = 2 * half
         self.paired = group >= 4
 
@@ -164,7 +164,7 @@
         p, n = place[axis], counts[axis]
         if full:
             steps = []
-            for k in sorted(range(1, n), key=lambda k: min(k, n - k)):
+            for k in sorted(range(1, n), key=lambda k: -k):
                 to, source = lax.rem(p + k, n), lax.rem(p + n - k, n)
                 steps.append((to, None, source, None, p, source))
             return steps
@@ -386,19 +386,19 @@
         for kz, mz in ((14.0 / 3.0, 8.0 / 30.0), (16.0 / 3.0, 16.0 / 30.0)):
             inv.append((FIRST / UNIT) / (kx * my * mz + mx * ky * mz + mx * my * kz))
 
-        def one(t):
-            gx = x_first + t * lv.group + xx
+        def one(i):
+            gx = x_first + (i - lv.pad) * lv.group + xx
             ok = jnp.where(y_ok & (gx >= 0) & (gx < n_x), 1.0, 0.0).astype(F32)
-            mk[t] = ok
-            iv[t, 0] = inv[0] * ok
-            iv[t, 1] = inv[1] * ok
-
-        loop(lv.tiles, one)
+            mk[i] = ok
+            iv[i, 0] = inv[0] * ok
+            iv[i, 1] = inv[1] * ok
+
+        loop(lv.tiles + 2 * lv.pad, one, 16)
         for par in range(2):
             gz = z_first + 2 * row + par
             zm[par] = jnp.where((gz >= 0) & (gz < n_z), 1.0, 0.0).astype(F32)
-        d[0] = jnp.zeros_like(d[0])
-        d[lv.tiles + 1] = jnp.zeros_like(d[0])
+        zero(d, slice(0, lv.pad))
+        zero(d, slice(lv.tiles + lv.pad, lv.tiles + 2 * lv.pad))
         ss[:, :, 0:8] = jnp.zeros_like(ss[:, :, 0:8])
         ss[:, :, 8 + lv.half :] = jnp.zeros_like(ss[:, :, 8 + lv.half :])
 
@@ -416,8 +416,9 @@
         lv2, 2, iv2, mk2, zm2, d2, ss2, start_x * (cx // 2), start_y * (cy // 2),
         iz * (cz // 2) - ZR // 2, lambda n: n // yh2, lambda n: n % yh2,
     )
-    c1[0:2] = jnp.zeros_like(c1[0:2])
-    c1[lv1.tiles + 2 :] = jnp.zeros_like(c1[0:2])
+    for ref in (r1, acc1):
+        zero(ref, slice(0, lv1.pad))
+        zero(ref, slice(lv1.tiles + lv1.pad, lv1.tiles + 2 * lv1.pad))
     xs1[:, 0:8] = jnp.zeros_like(xs1[:, 0:8])
     xs1[:, 8 + lv1.half :] = jnp.zeros_like(xs1[:, 8 + lv1.half :])
     up2[...] = jnp.zeros_like(up2)
@@ -468,15 +469,16 @@
             for s in range(0, lv.rows, step):
                 rows = slice(s, s + step)
                 if lv.paired:
-                    v = jnp.where(low, d[t + 1, rows], d[t, rows])
+                    v = jnp.where(low, d[t + lv.pad, rows], d[t + lv.pad - 1, rows])
                 else:
-                    v = d[t, rows]
-                hh[t, rows], hl[t, rows] = split(v)
+                    v = d[t + lv.pad - 1, rows]
+                hh[t + lv.pad, rows], hl[t + lv.pad, rows] = split(v)
 
         loop(count + (1 if lv.paired else 2), one)
 
-    def sweep(lv, hh, hl, w, ss, zm, lo, count, use):
-        chunk = 24 if lv.half % 24 == 0 else 32
+    def sweep(lv, hh, hl, w, ss, zm, lo, count, use, r_lo=0, r_hi=None):
+        r_hi = lv.half if r_hi is None else r_hi
+        chunk = next(c for c in (32, 24, 28, 8) if (r_hi - r_lo) % c == 0)
         n_cat = 2 if lv.paired else 3
         size = 2 if count % 2 == 0 else 1
 
@@ -485,7 +487,7 @@
 
             def lhs(h):
                 return jnp.concatenate(
-                    [h[pl.ds(t0 + j, size)].reshape(size * lv.rows, LANES) for j in range(n_cat)],
+                    [h[pl.ds(t0 + j + lv.pad, size)].reshape(size * lv.rows, LANES) for j in range(n_cat)],
                     axis=1,
                 )
 
@@ -501,7 +503,7 @@
                             at : at + lv.half, LANES * c : LANES * c + LANES
                         ]
                 t = t0 + k
-                for at in range(0, lv.half, chunk):
+                for at in range(r_lo, r_hi, chunk):
 
                     def rows_of(n, shift=0):
                         return ss[slot, n, pl.ds(8 + at + shift, chunk)]
@@ -545,7 +547,7 @@
         for par in range(2):
             for at in range(0, lv0.half, size):
                 rows = slice(par * lv0.half + at, par * lv0.half + at + size)
-                d = wide(iv0[t, par], size) * r0[t, rows] * zm0[par, at : at + size]
+                d = wide(iv0[t + 1, par], size) * r0[t, rows] * zm0[par, at : at + size]
                 if own(t):
                     acc0[t - own_lo, rows] = d0[t + 1, rows] + d
                 d0[t + 1, rows] = d
@@ -554,14 +556,14 @@
         r = r0[t, rows] - av
         r0[t, rows] = r
         d = KEEP * d0[t + 1, rows] + masked(
-            (RATIO * wide(iv0[t, par], n_rows(rows))) * r, edge
+            (RATIO * wide(iv0[t + 1, par], n_rows(rows))) * r, edge
         )
         if own(t):
             acc0[t - own_lo, rows] += d
         d0[t + 1, rows] = d
 
     def use_down(t, par, rows, av, edge):
-        r0[t, rows] = masked((r0[t, rows] - av) * wide(mk0[t], n_rows(rows)), edge)
+        r0[t, rows] = masked((r0[t, rows] - av) * wide(mk0[t + 1], n_rows(rows)), edge)
 
     lo_a, n_a = reach(6, 5)
     lo_b, n_b = reach(4, 3)
@@ -621,15 +623,15 @@
         )
 
     sources = [(None, own_x)] + [(st[3], st[5]) for st in x_steps]
-    for n, st in enumerate(x_steps):
-        when(st[1], lambda: g_copy(n).start())
+    for n in reversed(range(len(x_steps))):
+        when(x_steps[n][1], lambda: g_copy(n).start())
     for m, (ok, jx) in enumerate(sources):
 
         def act():
             if m:
                 g_copy(m - 1).wait_recv()
-            for n, st in enumerate(plane_steps):
-                when(st[1], lambda: p_copy(n, m, jx).start())
+            for n in reversed(range(len(plane_steps))):
+                when(plane_steps[n][1], lambda: p_copy(n, m, jx).start())
             land[own_y, jx, zq : zq + half_c] = packed if m == 0 else line[jx]
 
         when(ok, act)
@@ -651,10 +653,10 @@
                     else:
                         val = jnp.where(lane_h == jy, v, val)
                 rows = slice(par * lv1.half, par * lv1.half + lv1.half)
-                r1[t, rows] = val
-                d = (wide(iv1[t, par], lv1.half) * zm1[par]) * val
-                d1[t + 1, rows] = d
-                acc1[t, rows] = d
+                r1[t + lv1.pad, rows] = val
+                d = (wide(iv1[t + lv1.pad, par], lv1.half) * zm1[par]) * val
+                d1[t + lv1.pad, rows] = d
+                acc1[t + lv1.pad, rows] = d
 
     for m, (ok, jx) in enumerate(sources):
 
@@ -666,22 +668,25 @@
         place_block(jx)
 
     def use_step1(t, par, rows, av, edge):
-        r = r1[t, rows] - av
-        r1[t, rows] = r
-        d = KEEP * d1[t + 1, rows] + masked(
-            (RATIO * wide(iv1[t, par], n_rows(rows))) * r, edge
-        )
-        d1[t + 1, rows] = d
-        acc1[t, rows] += d
+        r = r1[t + lv1.pad, rows] - av
+        r1[t + lv1.pad, rows] = r
+        d = KEEP * d1[t + lv1.pad, rows] + masked(
+            (RATIO * wide(iv1[t + lv1.pad, par], n_rows(rows))) * r, edge
+        )
+        d1[t + lv1.pad, rows] = d
+        acc1[t + lv1.pad, rows] += d
 
     def use_down1(t, par, rows, av, edge):
-        r1[t, rows] = masked((r1[t, rows] - av) * wide(mk1[t], n_rows(rows)), edge)
+        r1[t + lv1.pad, rows] = masked((r1[t + lv1.pad, rows] - av) * wide(mk1[t + lv1.pad], n_rows(rows)), edge)
 
     n1 = lv1.tiles
     stage(lv1, d1, hh1, hl1, 0, n1)
-    sweep(lv1, hh1, hl1, weights('wa1'), ss1, zm1, 0, n1, use_step1)
+    z_cut = ZR // 4
+    sweep(lv1, hh1, hl1, weights('wa1'), ss1, zm1, 0, n1, use_step1, z_cut)
     stage(lv1, d1, hh1, hl1, 0, n1)
-    sweep(lv1, hh1, hl1, weights('wa1'), ss1, zm1, 0, n1, use_down1)
+    sweep(
+        lv1, hh1, hl1, weights('wa1'), ss1, zm1, 0, n1, use_down1, z_cut, lv1.half - z_cut
+    )
 
     ratio = 2 * lv2.group // lv1.group
     r_lo = (-3) // lv1.group
@@ -691,18 +696,18 @@
         a, e = max(0, ratio * t + r_lo), min(n1 - 1, ratio * t + r_hi)
         skip = (a - (ratio * t + r_lo)) * LANES
         x = restricted(
-            [r1[i] for i in range(a, e + 1)], wr1[skip : skip + (e + 1 - a) * LANES]
+            [r1[i + lv1.pad] for i in range(a, e + 1)], wr1[skip : skip + (e + 1 - a) * LANES]
         )
         xs1[0, 8 : 8 + lv1.half] = x[: lv1.half]
         xs1[1, 8 : 8 + lv1.half] = x[lv1.half :]
         for par, val in enumerate(z_restricted(xs1, 8, 7, lv2.half)):
             rows = slice(par * lv2.half, par * lv2.half + lv2.half)
             r2[t, rows] = val
-            d2[t + 1, rows] = (wide(iv2[t, par], lv2.half) * zm2[par]) * val
+            d2[t + 1, rows] = (wide(iv2[t + 1, par], lv2.half) * zm2[par]) * val
 
     def use_last(t, par, rows, av, edge):
         r = r2[t, rows] - av
-        step = masked((RATIO * wide(iv2[t, par], n_rows(rows))) * r, edge)
+        step = masked((RATIO * wide(iv2[t + 1, par], n_rows(rows))) * r, edge)
         lo = rows.start - par * lv2.half
         up2[t, par, lo : lo + n_rows(rows)] = (1.0 + KEEP) * d2[t + 1, rows] + step
 
@@ -734,31 +739,43 @@
                 for par in range(2):
                     rows = slice(par * lv1.half, par * lv1.half + lv1.half)
                     v = e[rows, LANES * k : LANES * k + LANES] * (
-                        wide(mk1[to], lv1.half) * zm1[par]
+                        wide(mk1[to + lv1.pad], lv1.half) * zm1[par]
                     )
-                    d1[to + 1, rows] = v
-                    acc1[to, rows] += v
+                    d1[to + lv1.pad, rows] = v
+                    acc1[to + lv1.pad, rows] += v
 
     def use_up1(t, par, rows, av, edge):
-        r = r1[t, rows] - av
-        r1[t, rows] = r
-        d1[t + 1, rows] = masked(wide(iv1[t, par], n_rows(rows)) * r, edge)
+        r = r1[t + lv1.pad, rows] - av
+        r1[t + lv1.pad, rows] = r
+        d1[t + lv1.pad, rows] = masked(wide(iv1[t + lv1.pad, par], n_rows(rows)) * r, edge)
 
     def use_final1(t, par, rows, av, edge):
-        r = r1[t, rows] - av
-        c1[t + 2, rows] = (acc1[t, rows] + (1.0 + KEEP) * d1[t + 1, rows]) + masked(
-            (RATIO * wide(iv1[t, par], n_rows(rows))) * r, edge
-        )
-
-    stage(lv1, d1, hh1, hl1, 0, n1)
-    sweep(lv1, hh1, hl1, weights('wa1'), ss1, zm1, 0, n1, use_up1)
-    stage(lv1, d1, hh1, hl1, 0, n1)
-    sweep(lv1, hh1, hl1, weights('wa1'), ss1, zm1, 0, n1, use_final1)
+        r = r1[t + lv1.pad, rows] - av
+        c1[t + lv1.pad, rows] = (acc1[t + lv1.pad, rows] + (1.0 + KEEP) * d1[t + lv1.pad, rows]) + masked(
+            (RATIO * wide(iv1[t + lv1.pad, par], n_rows(rows))) * r, edge
+        )
+
+    base1 = own_x * per
+
+    def around(reach):
+        lo, hi = (-reach) // lv1.group, (cx + reach) // lv1.group
+        return lo, hi + 1 - lo
+
+    up_lo, up_n = around(4)
+    if up_n % 2:
+        up_lo, up_n = up_lo - 1, up_n + 1
+    fin_lo, fin_n = around(2)
+    for lo, n, use in ((up_lo, up_n, use_up1), (fin_lo, fin_n, use_final1)):
+        stage(lv1, d1, hh1, hl1, base1 + lo, n)
+        sweep(
+            lv1, hh1, hl1, weights('wa1'), ss1, zm1, base1 + lo, n, use, z_cut,
+            lv1.half - z_cut,
+        )
 
     up = 2 * lv1.group // lv0.group
     tau_lo = (lo_b - own_lo) // up
     tau_hi = (lo_b + n_b - 1 - own_lo) // up
-    n_tau = tau_hi + 2 - tau_lo
+    n_tau = fin_lo + fin_n - tau_lo
     jn = (lv0.half // 2 + 7) // 8 * 8
     lane_j = lax.broadcasted_iota(jnp.int32, (jn, LANES), 1) // gs
     bad = ((lane_j == 0) & (own_y == 0)) | ((lane_j == 2) & (own_y == wy - 1))
@@ -766,7 +783,7 @@
     first = ZR // 2 - zh // 2
     wp0 = weights('wp0')
     for i in range(n_tau):
-        at = own_x * per + (tau_lo + i + 2)
+        at = base1 + (tau_lo + i + lv1.pad)
 
         def rows_of(par, start):
             v = pltpu.roll(c1[at, pl.ds(par * lv1.half + start, jn)], turn, 1)
@@ -778,12 +795,14 @@
         zp0[i, pl.ds(lv0.half, jn, stride=2)] = 0.375 * e2 + 0.75 * o2 - 0.125 * e3
         zp0[i, pl.ds(lv0.half + 1, jn, stride=2)] = 0.75 * o2 + 0.375 * e3 - 0.125 * e2
         zh0[i], zl0[i] = split(zp0[i, 0 : lv0.rows])
-    for i in range(n_tau - 1):
+    for i in range(tau_hi + 1 - tau_lo):
+        n_in = min(2, n_tau - i)
+        w = wp0[: n_in * LANES]
         e = jnp.dot(
-            jnp.concatenate([zh0[i], zh0[i + 1]], axis=1), wp0,
+            jnp.concatenate([zh0[i + j] for j in range(n_in)], axis=1), w,
             preferred_element_type=F32,
         ) + jnp.dot(
-            jnp.concatenate([zl0[i], zl0[i + 1]], axis=1), wp0,
+            jnp.concatenate([zl0[i + j] for j in range(n_in)], axis=1), w,
             preferred_element_type=F32,
         )
         for k in range(up):
@@ -792,7 +811,7 @@
                 for par in range(2):
                     rows = slice(par * lv0.half, par * lv0.half + lv0.half)
                     v = e[rows, LANES * k : LANES * k + LANES] * (
-                        wide(mk0[t], lv0.half) * zm0[par]
+                        wide(mk0[t + 1], lv0.half) * zm0[par]
                     )
                     d0[t + 1, rows] = v
                     if own(t):
@@ -801,19 +820,21 @@
     def use_up(t, par, rows, av, edge):
         r = r0[t, rows] - av
         r0[t, rows] = r
-        d0[t + 1, rows] = masked(wide(iv0[t, par], n_rows(rows)) * r, edge)
+        d0[t + 1, rows] = masked(wide(iv0[t + 1, par], n_rows(rows)) * r, edge)
 
     def use_final(t, par, rows, av, edge):
         r = r0[t, rows] - av
         acc0[t - own_lo, rows] += (1.0 + KEEP) * d0[t + 1, rows] + (
-            RATIO * wide(iv0[t, par], n_rows(rows))
+            RATIO * wide(iv0[t + 1, par], n_rows(rows))
         ) * r
 
     lo_c, n_c = reach(2, 1)
     stage(lv0, d0, hh0, hl0, lo_c, n_c)
     sweep(lv0, hh0, hl0, weights('wa0'), ss0, zm0, lo_c, n_c, use_up)
     stage(lv0, d0, hh0, hl0, own_lo, own_n)
-    sweep(lv0, hh0, hl0, weights('wa0'), ss0, zm0, own_lo, own_n, use_final)
+    sweep(
+        lv0, hh0, hl0, weights('wa0'), ss0, zm0, own_lo, own_n, use_final, zh, zh + hb
+    )
 
     for i in range(own_n):
         for par in range(2):
@@ -850,19 +871,19 @@
     yh0 = by + 2 * H
     xg0 = LANES // yh0
     lv0 = Level(
-        xg0, (bx + 2 * H) // xg0, yh0, (bz + 2 * H) // 2, lambda x, y: x * yh0 + y, H // 2
+        xg0, (bx + 2 * H) // xg0, yh0, (bz + 2 * H) // 2, lambda x, y: x * yh0 + y, H // 2, 1
     )
     xg1 = gs // cy
     lv1 = Level(
         xg1, cx * wx // xg1, cy * wy, (cz + 2 * ZR) // 2,
-        lambda x, y: (y // cy) * gs + x * cy + y % cy, ZR // 2,
+        lambda x, y: (y // cy) * gs + x * cy + y % cy, ZR // 2, 4,
     )
     y2 = cy * wy // 2
     yh2 = 16 if y2 <= 16 else 32
     xg2 = LANES // yh2
     lv2 = Level(
         xg2, -(-(cx * wx // 2) // xg2), y2, (cz + 2 * ZR) // 4, lambda x, y: x * yh2 + y,
-        ZR // 4,
+        ZR // 4, 1,
     )
 
     own_lo = H // xg0
@@ -936,11 +957,12 @@
     dma = lambda *s: pltpu.SemaphoreType.DMA(s)
 
     def per_level(lv):
-        t, n = lv.tiles, lv.rows
+        t, n, p = lv.tiles, lv.rows, lv.pad
         return (
-            vm(t + 2, n, LANES), vm(t, n, LANES), vm(t, n, LANES),
-            bm(t + 2, n, LANES), bm(t + 2, n, LANES), vm(4, 4, lv.half + 16, LANES),
-            vm(t, 2, 8, LANES), vm(t, 8, LANES), vm(2, lv.half, LANES),
+            vm(t + 2 * p, n, LANES), vm(t + 2 * p, n, LANES), vm(t + 2 * p, n, LANES),
+            bm(t + 2 * p + 2, n, LANES), bm(t + 2 * p + 2, n, LANES),
+            vm(4, 4, lv.half + 16, LANES), vm(t + 2 * p, 2, 8, LANES),
+            vm(t + 2 * p, 8, LANES), vm(2, lv.half, LANES),
         )
 
     p0, p1, p2 = per_level(lv0), per_level(lv1), per_level(lv2)
@@ -964,7 +986,7 @@
             vm(bx + 2 * H, yh0, bz), vm(bx + 2 * H, yh0, bz), vm(bz, LANES),
             vm(xg0, yh0, bz), vm(2, 3, 2, bx // xg0, H, LANES),
             vm(2, 3, 2, lv0.tiles, H, LANES),
-            *p0, *p1, vm(lv1.tiles + 4, lv1.rows, LANES), p2[0], p2[1], *p2[3:],
+            *p0, *p1, vm(lv1.tiles + 8, lv1.rows, LANES), p2[0], p2[1], *p2[3:],
             vm(2, lv0.half, LANES), vm(2, lv1.half + 16, LANES), vm(cz // 2, LANES),
             vm(wx, cz // 2, LANES), vm(wy, wx, lv1.half, LANES),
             vm(lv2.tiles, 2, lv2.half + 8, LANES), vm(lv2.tiles, lv1.rows, LANES),

time: 27.8 us -> 26.7 us (0.960)
  Pallas kernels: 27 us -> 25.9 us
    pallas_call x1, Pallas kernels: 27 us -> 25.9 us  [local(): pl.pallas_call(functools.partial(kernel, geo, lv0, lv1, lv2, parts), out_...]
where the time goes in v4:
time: 26.7 us; the launch traced here: 26.6 us
  Pallas kernels  25.9 us (97%)
  local copies, waits for them, and re-layouts  0.66 us (2%)
    pallas_call x1, Pallas kernels, local(): pl.pallas_call(functools.partial(kernel, geo, lv0, lv1, lv2, parts), out_...  25.9 us
    unnamed x1, local copies, waits for them, and re-layouts  0.66 us

profile of v4, /device:TPU:0, one launch (start us, length us, event | category | flops | bytes accessed | tf_op | source)
XLA Modules:
  0.0 26.6 jit_solution(11675125612941995363)
XLA Ops:
  0.0 25.9 %shard_map.37 = f32[16,16,128]{2,1,0:T(8,128)S(1)} custom-call(f32[16,16,128]{2,1,0:T(8,128)} %u_hbm.1, f32[16,16,128]{2,1,0:T(8,128)} %b_hbm.1, bf16[2304,256]{1,0:T(8,128)(2,1)} %constant.2.clone.w_hbm), custom_call_target="tpu_custom_call" | custom-call | tf_op jit(solution)/shard_map/pallas_call | solution.py:979
  25.9 0.7 %copy.5 = f32[16,16,128]{2,1,0:T(8,128)} copy(f32[16,16,128]{2,1,0:T(8,128)S(1)} %shard_map.37) | data formatting | bytes 262144

commit v5 on v4

--- a/solution.py
+++ b/solution.py
@@ -611,6 +611,18 @@
         st = x_steps[n]
         return remote(blk, line.at[st[4]], gsend.at[n], grecv.at[n], (st[0], iy, iz))
 
+    sources = [(None, own_x)] + [(st[3], st[5]) for st in x_steps]
+
+    step_rows = sum(half_c if st[4] is None else zq for st in plane_steps)
+    merged = (
+        full_x and full_y and nz <= 2 and step_rows > 0 and step_rows % yh0 == 0
+        and (step_rows // yh0) * len(sources) <= bx + 2 * H
+    )
+
+    def all_of(sem, steps):
+        ref = ue.at[0 : steps * step_rows // yh0]
+        return pltpu.make_async_copy(ref, ref, sem)
+
     def p_copy(n, m, jx):
         to, _, _, jy, zs = plane_steps[n]
         if zs is None:
@@ -619,10 +631,11 @@
             src, dst = pl.ds(zs[5], zq), pl.ds(zs[6], zq)
         from_ref = blk if m == 0 else line.at[jx]
         return remote(
-            from_ref.at[src], land.at[jy, jx, dst], psend.at[n, m], precv.at[n, m], to
-        )
-
-    sources = [(None, own_x)] + [(st[3], st[5]) for st in x_steps]
+            from_ref.at[src], land.at[jy, jx, dst],
+            psend.at[0, 0] if merged else psend.at[n, m],
+            precv.at[0, m] if merged else precv.at[n, m], to,
+        )
+
     for n in reversed(range(len(x_steps))):
         when(x_steps[n][1], lambda: g_copy(n).start())
     for m, (ok, jx) in enumerate(sources):
@@ -635,6 +648,13 @@
             land[own_y, jx, zq : zq + half_c] = packed if m == 0 else line[jx]
 
         when(ok, act)
+    for n, off in enumerate(xy_offs):
+        for k in range(2):
+            when(xy_step(off)[1], lambda: halo_copy(n, k).wait_send())
+    for m in range(len(z_steps)):
+        for n in range(len(spots)):
+            when(strip_ok(n, m, 1), lambda: strip_copy(n, m).wait_send())
+
     per = cx // lv1.group
     lane_h = lax.broadcasted_iota(jnp.int32, (lv1.half, LANES), 1) // gs
 
@@ -661,6 +681,9 @@
     for m, (ok, jx) in enumerate(sources):
 
         def act():
+            if merged:
+                all_of(precv.at[0, m], 1).wait()
+                return
             for n, st in enumerate(plane_steps):
                 when(st[2], lambda: p_copy(n, m, jx).wait_recv())
 
@@ -843,21 +866,18 @@
         v = tmp[...].T.reshape(lv0.group, yh0, bz)
         out_ref[lv0.group * i : lv0.group * i + lv0.group] = v[:, H : H + by]
 
-    for n, off in enumerate(xy_offs):
-        for k in range(2):
-            when(xy_step(off)[1], lambda: halo_copy(n, k).wait_send())
-    for m in range(len(z_steps)):
-        for n in range(len(spots)):
-            when(strip_ok(n, m, 1), lambda: strip_copy(n, m).wait_send())
     for n, st in enumerate(x_steps):
         when(st[1], lambda: g_copy(n).wait_send())
+    if merged:
+        all_of(psend.at[0, 0], len(sources)).wait()
     for m, (ok, jx) in enumerate(sources):
 
         def act():
             for n, st in enumerate(plane_steps):
                 when(st[1], lambda: p_copy(n, m, jx).wait_send())
 
-        when(ok, act)
+        if not merged:
+            when(ok, act)
 
 
 def local(mesh_shape, u, b):
@@ -976,6 +996,12 @@
     n_y = ny - 1 if wy == ny else 2 * REACH
     n_p = max(1, (n_y + 1) * (n_z + 1) - 1)
     n_xy, n_s = max(1, near * side - 1), near * side
+    step_rows = n_y * (cz // 2) + (n_y + 1) * n_z * (ZR // 2)
+    merged = (
+        wx == nx and wy == ny and nz <= 2 and step_rows > 0 and step_rows % yh0 == 0
+        and (step_rows // yh0) * nx <= bx + 2 * H
+    )
+    sems = (dma(1, 1), dma(1, nx)) if merged else (dma(n_p, n_x + 1), dma(n_p, n_x + 1))
     return pl.pallas_call(
         functools.partial(kernel, geo, lv0, lv1, lv2, parts),
         out_shape=pltpu.VMEM(u.shape, F32),
@@ -994,7 +1020,7 @@
             bm(lv2.tiles, lv1.rows, LANES), bm(lv2.tiles, lv1.rows, LANES),
             bm(n_tau, lv0.rows, LANES), bm(n_tau, lv0.rows, LANES),
             dma(3), dma(n_xy, 2), dma(n_xy, 2), dma(n_s, max(1, n_z)), dma(n_s, max(1, n_z)),
-            dma(n_x), dma(n_x), dma(n_p, n_x + 1), dma(n_p, n_x + 1),
+            dma(n_x), dma(n_x), *sems,
         ],
         compiler_params=pltpu.CompilerParams(
             collective_id=0, has_side_effects=True, vmem_limit_bytes=60 * 1024 * 1024

time: 26.7 us -> 26.2 us (0.981)
  Pallas kernels: 25.9 us -> 25.4 us
    pallas_call x1, Pallas kernels: 25.9 us -> 25.4 us  [local(): pl.pallas_call(functools.partial(kernel, geo, lv0, lv1, lv2, parts), out_...]
where the time goes in v5:
time: 26.2 us; the launch traced here: 26.1 us
  Pallas kernels  25.4 us (97%)
  local copies, waits for them, and re-layouts  0.66 us (3%)
    pallas_call x1, Pallas kernels, local(): pl.pallas_call(functools.partial(kernel, geo, lv0, lv1, lv2, parts), out_...  25.4 us
    unnamed x1, local copies, waits for them, and re-layouts  0.66 us

profile of v5, /device:TPU:0, one launch (start us, length us, event | category | flops | bytes accessed | tf_op | source)
XLA Modules:
  0.0 26.1 jit_solution(11874501690766333155)
XLA Ops:
  0.0 25.4 %shard_map.37 = f32[16,16,128]{2,1,0:T(8,128)S(1)} custom-call(f32[16,16,128]{2,1,0:T(8,128)} %u_hbm.1, f32[16,16,128]{2,1,0:T(8,128)} %b_hbm.1, bf16[2304,256]{1,0:T(8,128)(2,1)} %constant.2.clone.w_hbm), custom_call_target="tpu_custom_call" | custom-call | tf_op jit(solution)/shard_map/pallas_call | solution.py:1005
  25.4 0.7 %copy.5 = f32[16,16,128]{2,1,0:T(8,128)} copy(f32[16,16,128]{2,1,0:T(8,128)S(1)} %shard_map.37) | data formatting | bytes 262144
